TPU v7x, 16 devices: a whole 2x2x2 slice. The times are simulated.
16 devices in a mesh: model: 2 (over z), data: 8 (over y, x, core).
Axes of the slice: x: 2, y: 2, z: 2, core: 2. Of those that a mesh axis runs over, the one named last changes fastest.
Arguments:
- local_grads: bfloat16 [8, 384, 65536], P('data', None, 'model')
- master: float32 [384, 65536], P(None, ('model', 'data'))
- moment_one: float32 [384, 65536], P(None, ('model', 'data'))
- moment_two: float32 [384, 65536], P(None, ('model', 'data'))
Outputs:
- output 1: bfloat16 [384, 65536], P(None, 'model')
- output 2: float32 [384, 65536], P(None, ('model', 'data'))
- output 3: float32 [384, 65536], P(None, ('model', 'data'))
- output 4: float32 [384, 65536], P(None, ('model', 'data'))
All inputs are finite; a program needn't handle non-finite values.
Results may differ from a plain program's by a relative error of at most 0.001.
Values are sent between devices in bfloat16 or wider.
A program may use at most 1 GiB of HBM per device.

v0:
```python
import jax
import jax.numpy as jnp
from jax import lax
from jax.experimental import pallas as pl
from jax.experimental.pallas import tpu as pltpu
from jax.sharding import PartitionSpec as P

STEP = 4
LEARN_RATE = 0.08
BETA_ONE = 0.9
BETA_TWO = 0.999
EPSILON = 1e-6
WEIGHT_DECAY = 0.01
MAX_NORM = 1.0
CORR_ONE = 1.0 - BETA_ONE ** STEP
CORR_TWO = 1.0 - BETA_TWO ** STEP

ROWS = 384
HALF = 192
COLS = 4096
DATA = 8
DEVICES = 16
PIECE = 1024
PIECES = COLS // PIECE

RS_SIZES = (48, 48, 48, 32, 16)
RS_CHUNKS = len(RS_SIZES)
RS_STARTS = tuple(sum(RS_SIZES[:i]) for i in range(RS_CHUNKS))
AG_SIZES = (16,) + (32,) * 11 + (16,)
AG_CHUNKS = len(AG_SIZES)
AG_STARTS = tuple(sum(AG_SIZES[:i]) for i in range(AG_CHUNKS))
NORM_CHUNKS = ((0, 16), (16, 112), (112, 384))
OUT_PARTS = 4

MESH = pl.DeviceIdType.MESH
F32 = jnp.float32
BF16 = jnp.bfloat16


def fold_lanes(values):
    total = values[:, 0:128]
    for group in range(1, values.shape[1] // 128):
        total = total + values[:, group * 128:(group + 1) * 128]
    return total


def tensor_total(tile):
    row = [tile[s:s + 1, :] for s in range(8)]
    first3 = row[0] + row[1] + row[2]
    first4 = first3 + row[3]
    mid3 = row[4] + row[5] + row[6]
    last4 = mid3 + row[7]
    sub = lax.broadcasted_iota(jnp.int32, (8, 128), 0)
    kind = lax.broadcasted_iota(jnp.int32, (8, 128), 1) % 3
    full = lambda value: jnp.broadcast_to(value, (8, 128))
    low = jnp.where(kind == 0, jnp.where(sub == 3, full(row[3]), full(first3)), full(first4))
    high = jnp.where(kind == 1, jnp.where(sub == 7, full(row[7]), full(mid3)), full(last4))
    return jnp.where(sub < 4, low, high)


def first_totals(row):
    lane = lax.broadcasted_iota(jnp.int32, (8, 128), 1)
    sub = lax.broadcasted_iota(jnp.int32, (8, 128), 0)
    tile = jnp.zeros((8, 128), F32)
    for group in range(NORM_CHUNKS[0][1] // 8):
        low, high = ((3, 4), (4, 7), (4, 8))[group % 3]
        part = lambda s: (s >= low).astype(jnp.int32) + (s >= high).astype(jnp.int32)
        same = (lane // 8 == group) & (part(sub) == part(lane % 8))
        total = jnp.sum(jnp.where(same, jnp.broadcast_to(row, (8, 128)), 0.0), axis=1, keepdims=True)
        tile = jnp.where(lane == group, total, tile)
    return tile


def kernel(grad_ref, master_ref, one_ref, two_ref, params, master, one, two, relay, grad, weight_buf, norm_buf, first_buf, sq_buf,
           load_sem, rs_recv, rs_send, hop_recv, hop_send, ex_recv, ex_send, ag_x, ag_y, ag_d, ag_o, ag_send):
    model = lax.axis_index("model")
    me = lax.axis_index("data")
    linear = model * DATA + me
    core = me % 2
    x = (me // 2) % 2
    y = me // 4
    to_core = 1 - 2 * core
    near_x = me + 2 - 4 * x
    near_y = me + 4 - 8 * y
    diag = near_x + 4 - 8 * y
    other = me + to_core
    peer = lambda index: {"model": model, "data": index}
    block = lambda index: pl.ds(pl.multiple_of(index * COLS, COLS), COLS)

    loads = [pltpu.make_async_copy(source, target, load_sem.at[i])
             for i, (source, target) in enumerate(((master_ref, master), (one_ref, one), (two_ref, two)))]

    first = (near_x, near_y)
    second = (near_y, near_x)

    def rows_of(half, chunk):
        return pl.ds(half * HALF + RS_STARTS[chunk], RS_SIZES[chunk])

    barrier = pltpu.get_barrier_semaphore()

    @pl.loop(1, DEVICES)
    def _(offset):
        index = (linear + offset) % DEVICES
        pl.semaphore_signal(barrier, inc=1, device_id={"model": index // DATA, "data": index % DATA}, device_id_type=MESH)

    for chunk in range(RS_CHUNKS):
        for half in range(2):
            rows = rows_of(half, chunk)
            for part, owner in enumerate((me, second[half])):
                pltpu.make_async_copy(grad_ref.at[0, rows, block(owner)], params.at[rows, pl.ds(part * COLS, COLS)], rs_recv.at[half, chunk]).start()
    for load in loads:
        load.start()

    pl.semaphore_wait(barrier, DEVICES - 1)

    def remote(source, target, send, recv, index):
        return pltpu.make_async_remote_copy(src_ref=source, dst_ref=target, send_sem=send, recv_sem=recv,
                                            device_id=peer(index), device_id_type=MESH)

    for chunk in range(RS_CHUNKS):
        for half in range(2):
            rows = rows_of(half, chunk)
            recv = rs_recv.at[half, chunk]
            send = rs_send.at[half]
            for turn in range(2):
                shift = turn * to_core
                for part, owner in enumerate((first[half] + shift, diag + shift)):
                    remote(grad_ref.at[0, rows, block(owner)], params.at[rows, pl.ds((4 + 2 * turn + part) * COLS, COLS)], send, recv, first[half] + shift).start()
            for part, owner in enumerate((other, second[half] + to_core)):
                remote(grad_ref.at[0, rows, block(owner)], params.at[rows, pl.ds((2 + part) * COLS, COLS)], send, recv, other).start()

    for load in loads:
        load.wait()

    lane = lax.broadcasted_iota(jnp.int32, (8, 128), 1)
    sub = lax.broadcasted_iota(jnp.int32, (8, 128), 0)

    def weight_rows(group, tile):
        rows = pl.ds(pl.multiple_of(group * 8, 8), 8)

        def piece(i, total):
            value = master[rows, pl.ds(pl.multiple_of(i * PIECE, PIECE), PIECE)]
            return total + fold_lanes(value * value)

        total = lax.fori_loop(0, PIECES, piece, jnp.zeros((8, 128), F32))
        return jnp.where(lane == group, jnp.sum(total, axis=1, keepdims=True), tile)

    weight_buf[linear] = lax.fori_loop(0, ROWS // 8, weight_rows, jnp.zeros((8, 128), F32))

    def exchange(buf, number):
        @pl.loop(1, DEVICES)
        def _(offset):
            index = (linear + offset) % DEVICES
            pltpu.make_async_remote_copy(src_ref=buf.at[linear], dst_ref=buf.at[linear], send_sem=ex_send.at[number], recv_sem=ex_recv.at[number],
                                         device_id={"model": index // DATA, "data": index % DATA}, device_id_type=MESH).start()

    def exchange_wait(buf, sem):
        others = buf.at[pl.ds(0, DEVICES - 1)]
        pltpu.make_async_copy(others, others, sem).wait()

    def gathered(buf):
        total = buf[0]
        for index in range(1, DEVICES):
            total = total + buf[index]
        return total

    EX_WEIGHT, EX_GRAD, EX_FIRST = range(3)

    def four(rows, cols_at, part):
        total = params[rows, pl.ds(pl.multiple_of(part * COLS + cols_at, PIECE), PIECE)].astype(F32)
        for source in range(1, 4):
            total = total + params[rows, pl.ds(pl.multiple_of((2 * source + part) * COLS + cols_at, PIECE), PIECE)].astype(F32)
        return total

    def hop(half, chunk):
        rows = rows_of(half, chunk)
        return remote(relay.at[rows], grad.at[rows], hop_send.at[half], hop_recv.at[half, chunk], second[half])

    for chunk in range(RS_CHUNKS):
        for half in range(2):
            rows = rows_of(half, chunk)
            whole = params.at[rows]
            pltpu.make_async_copy(whole, whole, rs_recv.at[half, chunk]).wait()

            @pl.loop(0, RS_SIZES[chunk] // 16 * PIECES)
            def _(step):
                tile_rows = pl.ds(pl.multiple_of(half * HALF + RS_STARTS[chunk] + step // PIECES * 16, 16), 16)
                cols_at = step % PIECES * PIECE
                relay[tile_rows, pl.ds(pl.multiple_of(cols_at, PIECE), PIECE)] = four(tile_rows, cols_at, 1)

            hop(half, chunk).start()
        if chunk == 0:
            exchange(weight_buf, EX_WEIGHT)

    square = jnp.zeros((8, 128), F32)
    for chunk in range(RS_CHUNKS):
        for half in range(2):
            hop(half, chunk).wait_recv()

            def finish(step, total):
                tile_rows = pl.ds(pl.multiple_of(half * HALF + RS_STARTS[chunk] + step // PIECES * 16, 16), 16)
                cols_at = step % PIECES * PIECE
                cols = pl.ds(pl.multiple_of(cols_at, PIECE), PIECE)
                value = (grad[tile_rows, cols] + four(tile_rows, cols_at, 0)) * (1.0 / DATA)
                grad[tile_rows, cols] = value
                folded = fold_lanes(value * value)
                return total + (folded[0:8] + folded[8:16])

            square = lax.fori_loop(0, RS_SIZES[chunk] // 16 * PIECES, finish, square)

    norm_buf[linear] = jnp.sum(square, axis=0, keepdims=True)
    exchange_wait(weight_buf, ex_recv.at[EX_WEIGHT])
    weight_norm = jnp.sqrt(tensor_total(gathered(weight_buf)))
    exchange(norm_buf, EX_GRAD)
    for half in range(2):
        rows = pl.ds(half * HALF, HALF)
        pltpu.make_async_copy(relay.at[rows], relay.at[rows], hop_send.at[half]).wait()
    exchange_wait(norm_buf, ex_recv.at[EX_GRAD])
    grad_norm = jnp.sqrt(jnp.sum(gathered(norm_buf), axis=1, keepdims=True))
    clip = jnp.minimum(1.0, MAX_NORM / grad_norm)

    def adam_row_sums(group):
        rows = pl.ds(pl.multiple_of(group * 8, 8), 8)

        def piece(i, total):
            cols = pl.ds(pl.multiple_of(i * PIECE, PIECE), PIECE)
            scaled = grad[rows, cols] * clip
            new_one = BETA_ONE * one[rows, cols] + (1.0 - BETA_ONE) * scaled
            new_two = BETA_TWO * two[rows, cols] + (1.0 - BETA_TWO) * (scaled * scaled)
            one[rows, cols] = new_one
            two[rows, cols] = new_two
            direction = (new_one * (1.0 / CORR_ONE)) / (jnp.sqrt(new_two * (1.0 / CORR_TWO)) + EPSILON) + WEIGHT_DECAY * master[rows, cols]
            relay[rows, cols] = direction
            return total + fold_lanes(direction * direction)

        total = lax.fori_loop(0, PIECES, piece, jnp.zeros((8, 128), F32))
        return jnp.sum(total, axis=1, keepdims=True)

    def adam_rows(group, tile):
        return jnp.where(lane == group, adam_row_sums(group), tile)

    def adam_first(group, tile):
        return jnp.where(lane == 8 * group + sub, adam_row_sums(group), tile)

    def step_rates(number):
        if number == 0:
            exchange_wait(first_buf, ex_recv.at[EX_FIRST])
            total = first_totals(gathered(first_buf))
        else:
            exchange_wait(sq_buf.at[number - 1], ex_recv.at[EX_FIRST + number])
            total = tensor_total(gathered(sq_buf.at[number - 1]))
        return weight_norm / jnp.sqrt(total) * LEARN_RATE

    def ag_rows(chunk):
        return pl.ds(AG_STARTS[chunk], AG_SIZES[chunk])

    def update(number, rates):
        start, stop = NORM_CHUNKS[number]
        for chunk in range(AG_CHUNKS):
            if not start <= AG_STARTS[chunk] < stop:
                continue

            @pl.loop(0, AG_SIZES[chunk] // 16)
            def _(tile):
                group = AG_STARTS[chunk] // 8 + 2 * tile
                rows = pl.ds(pl.multiple_of(AG_STARTS[chunk] + tile * 16, 16), 16)
                rate = jnp.concatenate([jnp.sum(jnp.where(lane == group + i, rates, 0.0), axis=1, keepdims=True) for i in range(2)], axis=0)

                @pl.loop(0, PIECES)
                def _(i):
                    cols = pl.ds(pl.multiple_of(i * PIECE, PIECE), PIECE)
                    value = master[rows, cols] - rate * relay[rows, cols]
                    master[rows, cols] = value
                    params[rows, pl.ds(pl.multiple_of(me * COLS + i * PIECE, PIECE), PIECE)] = value.astype(BF16)

            rows = ag_rows(chunk)
            own = params.at[rows, block(me)]
            remote(own, own, ag_send.at[0], ag_x.at[chunk], near_x).start()
            remote(own, own, ag_send.at[1], ag_y.at[chunk], near_y).start()
            remote(own, own, ag_send.at[2], ag_o, other).start()

    groups = [(start // 8, stop // 8) for start, stop in NORM_CHUNKS]
    zero_tile = jnp.zeros((8, 128), F32)
    first_buf[linear] = jnp.sum(lax.fori_loop(*groups[0], adam_first, zero_tile), axis=0, keepdims=True)
    tile = lax.fori_loop(groups[1][0], groups[1][0] + 1, adam_rows, zero_tile)
    exchange(first_buf, EX_FIRST)
    sq_buf[0, linear] = lax.fori_loop(groups[1][0] + 1, groups[1][1], adam_rows, tile)
    tile = lax.fori_loop(groups[2][0], groups[2][0] + 1, adam_rows, zero_tile)
    exchange(sq_buf.at[0], EX_FIRST + 1)
    update(0, step_rates(0))
    update(1, step_rates(1))
    sq_buf[1, linear] = lax.fori_loop(groups[2][0] + 1, groups[2][1], adam_rows, tile)
    exchange(sq_buf.at[1], EX_FIRST + 2)
    update(2, step_rates(2))

    def arrived(sem, source, rows):
        view = params.at[rows, block(source)]
        pltpu.make_async_copy(view, view, sem).wait()
        return view

    for chunk in range(AG_CHUNKS):
        rows = ag_rows(chunk)
        view = arrived(ag_x.at[chunk], near_x, rows)
        if chunk % 2 == 0:
            remote(view, view, ag_send.at[1], ag_d.at[chunk], near_y).start()
        remote(view, view, ag_send.at[2], ag_o, other).start()
        view = arrived(ag_y.at[chunk], near_y, rows)
        if chunk % 2 == 1:
            remote(view, view, ag_send.at[0], ag_d.at[chunk], near_x).start()
        remote(view, view, ag_send.at[2], ag_o, other).start()

    for chunk in range(AG_CHUNKS):
        view = arrived(ag_d.at[chunk], diag, ag_rows(chunk))
        remote(view, view, ag_send.at[2], ag_o, other).start()

    half_cols = params.at[:, pl.ds(0, DATA // 2 * COLS)]
    pltpu.make_async_copy(half_cols, half_cols, ag_o).wait()
    pltpu.make_async_copy(half_cols, half_cols, ag_send.at[2]).wait()
    for direction in range(2):
        for part in (pl.ds(0, ROWS), pl.ds(0, HALF)):
            view = params.at[part, pl.ds(0, COLS)]
            pltpu.make_async_copy(view, view, ag_send.at[direction]).wait()
    for half in range(2):
        view = params.at[pl.ds(0, HALF), pl.ds(0, 6 * COLS)]
        pltpu.make_async_copy(view, view, rs_send.at[half]).wait()
    exchange_wait(weight_buf, ex_send.at[EX_WEIGHT])
    exchange_wait(norm_buf, ex_send.at[EX_GRAD])
    exchange_wait(first_buf, ex_send.at[EX_FIRST])
    for number in range(2):
        exchange_wait(sq_buf.at[number], ex_send.at[EX_FIRST + 1 + number])


def write_out(*refs):
    count = len(refs) // 2
    sem = refs[-1]
    copies = []
    for source, target in zip(refs[:count], refs[count:-1]):
        for part in range(OUT_PARTS):
            rows = pl.ds(part * (ROWS // OUT_PARTS), ROWS // OUT_PARTS)
            copies.append(pltpu.make_async_copy(source.at[rows], target.at[rows], sem.at[len(copies)]))
    for copy in copies:
        copy.start()
    for copy in copies:
        copy.wait()


def solution(mesh):
    def device_step(local_grads, master, moment_one, moment_two):
        any_spec = pl.BlockSpec(memory_space=pl.ANY)
        vmem_spec = pl.BlockSpec(memory_space=pltpu.VMEM)
        state = pltpu.VMEM((ROWS, COLS), F32)
        dma = pltpu.SemaphoreType.DMA
        results = pl.pallas_call(
            kernel,
            name="lamb",
            out_shape=(pltpu.VMEM((ROWS, DATA * COLS), BF16), state, state, state),
            in_specs=[any_spec] * 4,
            out_specs=[vmem_spec] * 4,
            scratch_shapes=[
                pltpu.VMEM((ROWS, COLS), F32),
                pltpu.VMEM((ROWS, COLS), F32),
                pltpu.VMEM((DEVICES, 8, 128), F32),
                pltpu.VMEM((DEVICES, 1, 128), F32),
                pltpu.VMEM((DEVICES, 1, 128), F32),
                pltpu.VMEM((2, DEVICES, 8, 128), F32),
                dma((3,)),
                dma((2, RS_CHUNKS)),
                dma((2,)),
                dma((2, RS_CHUNKS)),
                dma((2,)),
                dma((5,)),
                dma((5,)),
                dma((AG_CHUNKS,)),
                dma((AG_CHUNKS,)),
                dma((AG_CHUNKS,)),
                dma,
                dma((3,)),
            ],
            compiler_params=pltpu.CompilerParams(collective_id=0, has_side_effects=True, vmem_limit_bytes=16 << 20),
        )(local_grads, master, moment_one, moment_two)
        written = []
        for group in (results[:1], results[1:]):
            written += pl.pallas_call(
                write_out,
                name="write_out",
                out_shape=[jax.ShapeDtypeStruct(value.shape, value.dtype) for value in group],
                in_specs=[vmem_spec] * len(group),
                out_specs=[any_spec] * len(group),
                scratch_shapes=[dma((len(group) * OUT_PARTS,))],
                compiler_params=pltpu.CompilerParams(vmem_limit_bytes=1 << 20),
            )(*group)
        return tuple(written)

    state_spec = P(None, ('model', 'data'))
    return jax.shard_map(device_step, mesh=mesh, in_specs=(P('data', None, 'model'), state_spec, state_spec, state_spec), out_specs=(P(None, 'model'), state_spec, state_spec, state_spec), check_vma=False)
```

profile of v0, /device:TPU:0, one launch (start us, length us, event | category | flops | bytes accessed | tf_op | source)
XLA Modules:
  0.0 344.6 jit_solution(11827915433060055878)
XLA Ops:
  0.6 328.8 %lamb.1 = (bf16[384,32768]{1,0:T(8,128)(2,1)S(1)}, f32[384,4096]{1,0:T(8,128)S(1)}, f32[384,4096]{1,0:T(8,128)S(1)}, f32[384,4096]{1,0:T(8,128)S(1)}) custom-call(bf16[1,384,32768]{2,1,0:T(8,128)(2,1)} %grad_ref.1, f32[384,4096]{1,0:T(8,128)} %master_ref.1, f32[384,4096]{1,0:T(8,128)} %one_ref.1, f32[384,4096]{1,0:T(8,128)} %two_ref.1), custom_call_target="tpu_custom_call" | custom-call | tf_op jit(solution)/shard_map/lamb/pallas_call | solution.py:353
  329.5 8.6 %write_out.2 = bf16[384,32768]{1,0:T(8,128)(2,1)} custom-call(bf16[384,32768]{1,0:T(8,128)(2,1)S(1)} %get-tuple-element.11.refs_0_), custom_call_target="tpu_custom_call" | custom-call | tf_op jit(solution)/shard_map/write_out/pallas_call | solution.py:383
  338.1 6.6 %write_out.3 = (f32[384,4096]{1,0:T(8,128)}, f32[384,4096]{1,0:T(8,128)}, f32[384,4096]{1,0:T(8,128)}) custom-call(f32[384,4096]{1,0:T(8,128)S(1)} %get-tuple-element.12.refs_0_, f32[384,4096]{1,0:T(8,128)S(1)} %get-tuple-element.13.refs_1_, f32[384,4096]{1,0:T(8,128)S(1)} %get-tuple-element.14.refs_2_), custom_call_target="tpu_custom_call" | custom-call | tf_op jit(solution)/shard_map/write_out/pallas_call | solution.py:383
where the time goes:
time: 345 us
  Pallas kernels  344 us (100%)
    pallas_call x1, Pallas kernels, device_step(): pl.pallas_call(kernel, name='lamb', out_shape=(pltpu.VMEM((ROWS, DATA * C...  329 us
    pallas_call x2, Pallas kernels, device_step(): pl.pallas_call(write_out, name='write_out', out_shape=[jax.ShapeDtypeStru...  15.2 us

commit v1 on v0

--- a/solution.py
+++ b/solution.py
@@ -103,14 +103,6 @@
         index = (linear + offset) % DEVICES
         pl.semaphore_signal(barrier, inc=1, device_id={"model": index // DATA, "data": index % DATA}, device_id_type=MESH)
 
-    for chunk in range(RS_CHUNKS):
-        for half in range(2):
-            rows = rows_of(half, chunk)
-            for part, owner in enumerate((me, second[half])):
-                pltpu.make_async_copy(grad_ref.at[0, rows, block(owner)], params.at[rows, pl.ds(part * COLS, COLS)], rs_recv.at[half, chunk]).start()
-    for load in loads:
-        load.start()
-
     pl.semaphore_wait(barrier, DEVICES - 1)
 
     def remote(source, target, send, recv, index):
@@ -129,8 +121,13 @@
             for part, owner in enumerate((other, second[half] + to_core)):
                 remote(grad_ref.at[0, rows, block(owner)], params.at[rows, pl.ds((2 + part) * COLS, COLS)], send, recv, other).start()
 
-    for load in loads:
-        load.wait()
+    def load_own(chunk):
+        for half in range(2):
+            rows = rows_of(half, chunk)
+            for part, owner in enumerate((me, second[half])):
+                pltpu.make_async_copy(grad_ref.at[0, rows, block(owner)], params.at[rows, pl.ds(part * COLS, COLS)], rs_recv.at[half, chunk]).start()
+
+    load_own(0)
 
     lane = lax.broadcasted_iota(jnp.int32, (8, 128), 1)
     sub = lax.broadcasted_iota(jnp.int32, (8, 128), 0)
@@ -145,7 +142,6 @@
         total = lax.fori_loop(0, PIECES, piece, jnp.zeros((8, 128), F32))
         return jnp.where(lane == group, jnp.sum(total, axis=1, keepdims=True), tile)
 
-    weight_buf[linear] = lax.fori_loop(0, ROWS // 8, weight_rows, jnp.zeros((8, 128), F32))
 
     def exchange(buf, number):
         @pl.loop(1, DEVICES)
@@ -189,7 +185,14 @@
                 relay[tile_rows, pl.ds(pl.multiple_of(cols_at, PIECE), PIECE)] = four(tile_rows, cols_at, 1)
 
             hop(half, chunk).start()
-        if chunk == 0:
+        if chunk + 1 < RS_CHUNKS:
+            load_own(chunk + 1)
+        if chunk < 3:
+            loads[chunk].start()
+        if chunk == 1:
+            loads[0].wait()
+            weight_buf[linear] = lax.fori_loop(0, ROWS // 8, weight_rows, jnp.zeros((8, 128), F32))
+        if chunk == 2:
             exchange(weight_buf, EX_WEIGHT)
 
     square = jnp.zeros((8, 128), F32)
@@ -215,6 +218,8 @@
     for half in range(2):
         rows = pl.ds(half * HALF, HALF)
         pltpu.make_async_copy(relay.at[rows], relay.at[rows], hop_send.at[half]).wait()
+    for load in loads[1:]:
+        load.wait()
     exchange_wait(norm_buf, ex_recv.at[EX_GRAD])
     grad_norm = jnp.sqrt(jnp.sum(gathered(norm_buf), axis=1, keepdims=True))
     clip = jnp.minimum(1.0, MAX_NORM / grad_norm)

time: 345 us -> 345 us (level)
  no operation moved by 1% of the time
where the time goes in v1:
time: 345 us
  Pallas kernels  344 us (100%)
    pallas_call x1, Pallas kernels, device_step(): pl.pallas_call(kernel, name='lamb', out_shape=(pltpu.VMEM((ROWS, DATA * C...  329 us
    pallas_call x2, Pallas kernels, device_step(): pl.pallas_call(write_out, name='write_out', out_shape=[jax.ShapeDtypeStru...  15.2 us

profile of v1, /device:TPU:0, one launch (start us, length us, event | category | flops | bytes accessed | tf_op | source)
XLA Modules:
  0.0 344.6 jit_solution(10311600052508885057)
XLA Ops:
  0.6 328.8 %lamb.1 = (bf16[384,32768]{1,0:T(8,128)(2,1)S(1)}, f32[384,4096]{1,0:T(8,128)S(1)}, f32[384,4096]{1,0:T(8,128)S(1)}, f32[384,4096]{1,0:T(8,128)S(1)}) custom-call(bf16[1,384,32768]{2,1,0:T(8,128)(2,1)} %grad_ref.1, f32[384,4096]{1,0:T(8,128)} %master_ref.1, f32[384,4096]{1,0:T(8,128)} %one_ref.1, f32[384,4096]{1,0:T(8,128)} %two_ref.1), custom_call_target="tpu_custom_call" | custom-call | tf_op jit(solution)/shard_map/lamb/pallas_call | solution.py:358
  329.4 8.6 %write_out.2 = bf16[384,32768]{1,0:T(8,128)(2,1)} custom-call(bf16[384,32768]{1,0:T(8,128)(2,1)S(1)} %get-tuple-element.11.refs_0_), custom_call_target="tpu_custom_call" | custom-call | tf_op jit(solution)/shard_map/write_out/pallas_call | solution.py:388
  338.0 6.6 %write_out.3 = (f32[384,4096]{1,0:T(8,128)}, f32[384,4096]{1,0:T(8,128)}, f32[384,4096]{1,0:T(8,128)}) custom-call(f32[384,4096]{1,0:T(8,128)S(1)} %get-tuple-element.12.refs_0_, f32[384,4096]{1,0:T(8,128)S(1)} %get-tuple-element.13.refs_1_, f32[384,4096]{1,0:T(8,128)S(1)} %get-tuple-element.14.refs_2_), custom_call_target="tpu_custom_call" | custom-call | tf_op jit(solution)/shard_map/write_out/pallas_call | solution.py:388

commit v2 on v1

--- a/solution.py
+++ b/solution.py
@@ -26,10 +26,10 @@
 RS_SIZES = (48, 48, 48, 32, 16)
 RS_CHUNKS = len(RS_SIZES)
 RS_STARTS = tuple(sum(RS_SIZES[:i]) for i in range(RS_CHUNKS))
-AG_SIZES = (16,) + (32,) * 11 + (16,)
+AG_SIZES = (32,) * 10 + (16,) * 4
 AG_CHUNKS = len(AG_SIZES)
 AG_STARTS = tuple(sum(AG_SIZES[:i]) for i in range(AG_CHUNKS))
-NORM_CHUNKS = ((0, 16), (16, 112), (112, 384))
+NORM_CHUNKS = ((0, 32), (32, 224), (224, 384))
 OUT_PARTS = 4
 
 MESH = pl.DeviceIdType.MESH
@@ -212,14 +212,14 @@
             square = lax.fori_loop(0, RS_SIZES[chunk] // 16 * PIECES, finish, square)
 
     norm_buf[linear] = jnp.sum(square, axis=0, keepdims=True)
-    exchange_wait(weight_buf, ex_recv.at[EX_WEIGHT])
-    weight_norm = jnp.sqrt(tensor_total(gathered(weight_buf)))
     exchange(norm_buf, EX_GRAD)
     for half in range(2):
         rows = pl.ds(half * HALF, HALF)
         pltpu.make_async_copy(relay.at[rows], relay.at[rows], hop_send.at[half]).wait()
     for load in loads[1:]:
         load.wait()
+    exchange_wait(weight_buf, ex_recv.at[EX_WEIGHT])
+    weight_norm = jnp.sqrt(tensor_total(gathered(weight_buf)))
     exchange_wait(norm_buf, ex_recv.at[EX_GRAD])
     grad_norm = jnp.sqrt(jnp.sum(gathered(norm_buf), axis=1, keepdims=True))
     clip = jnp.minimum(1.0, MAX_NORM / grad_norm)
@@ -293,9 +293,10 @@
     tile = lax.fori_loop(groups[2][0], groups[2][0] + 1, adam_rows, zero_tile)
     exchange(sq_buf.at[0], EX_FIRST + 1)
     update(0, step_rates(0))
-    update(1, step_rates(1))
     sq_buf[1, linear] = lax.fori_loop(groups[2][0] + 1, groups[2][1], adam_rows, tile)
+    rates = step_rates(1)
     exchange(sq_buf.at[1], EX_FIRST + 2)
+    update(1, rates)
     update(2, step_rates(2))
 
     def arrived(sem, source, rows):

time: 345 us -> 343 us (level)
  no operation moved by 1% of the time
where the time goes in v2:
time: 343 us
  Pallas kernels  343 us (100%)
    pallas_call x1, Pallas kernels, device_step(): pl.pallas_call(kernel, name='lamb', out_shape=(pltpu.VMEM((ROWS, DATA * C...  327 us
    pallas_call x2, Pallas kernels, device_step(): pl.pallas_call(write_out, name='write_out', out_shape=[jax.ShapeDtypeStru...  15.2 us

profile of v2, /device:TPU:0, one launch (start us, length us, event | category | flops | bytes accessed | tf_op | source)
XLA Modules:
  0.0 343.2 jit_solution(6894397595283198772)
XLA Ops:
  0.6 327.4 %lamb.1 = (bf16[384,32768]{1,0:T(8,128)(2,1)S(1)}, f32[384,4096]{1,0:T(8,128)S(1)}, f32[384,4096]{1,0:T(8,128)S(1)}, f32[384,4096]{1,0:T(8,128)S(1)}) custom-call(bf16[1,384,32768]{2,1,0:T(8,128)(2,1)} %grad_ref.1, f32[384,4096]{1,0:T(8,128)} %master_ref.1, f32[384,4096]{1,0:T(8,128)} %one_ref.1, f32[384,4096]{1,0:T(8,128)} %two_ref.1), custom_call_target="tpu_custom_call" | custom-call | tf_op jit(solution)/shard_map/lamb/pallas_call | solution.py:359
  328.0 8.6 %write_out.2 = bf16[384,32768]{1,0:T(8,128)(2,1)} custom-call(bf16[384,32768]{1,0:T(8,128)(2,1)S(1)} %get-tuple-element.11.refs_0_), custom_call_target="tpu_custom_call" | custom-call | tf_op jit(solution)/shard_map/write_out/pallas_call | solution.py:389
  336.6 6.6 %write_out.3 = (f32[384,4096]{1,0:T(8,128)}, f32[384,4096]{1,0:T(8,128)}, f32[384,4096]{1,0:T(8,128)}) custom-call(f32[384,4096]{1,0:T(8,128)S(1)} %get-tuple-element.12.refs_0_, f32[384,4096]{1,0:T(8,128)S(1)} %get-tuple-element.13.refs_1_, f32[384,4096]{1,0:T(8,128)S(1)} %get-tuple-element.14.refs_2_), custom_call_target="tpu_custom_call" | custom-call | tf_op jit(solution)/shard_map/write_out/pallas_call | solution.py:389

commit v3 on v2

--- a/solution.py
+++ b/solution.py
@@ -22,6 +22,7 @@
 DEVICES = 16
 PIECE = 1024
 PIECES = COLS // PIECE
+ADAM_PIECE = 1024
 
 RS_SIZES = (48, 48, 48, 32, 16)
 RS_CHUNKS = len(RS_SIZES)
@@ -29,7 +30,7 @@
 AG_SIZES = (32,) * 10 + (16,) * 4
 AG_CHUNKS = len(AG_SIZES)
 AG_STARTS = tuple(sum(AG_SIZES[:i]) for i in range(AG_CHUNKS))
-NORM_CHUNKS = ((0, 32), (32, 224), (224, 384))
+NORM_CHUNKS = ((0, 32), (32, 288), (288, 384))
 OUT_PARTS = 4
 
 MESH = pl.DeviceIdType.MESH
@@ -71,7 +72,7 @@
     return tile
 
 
-def kernel(grad_ref, master_ref, one_ref, two_ref, params, master, one, two, relay, grad, weight_buf, norm_buf, first_buf, sq_buf,
+def kernel(grad_ref, master_ref, one_ref, two_ref, params, master, one, two, relay, grad, weight_buf, norm_buf, first_buf, sq_buf, part_buf,
            load_sem, rs_recv, rs_send, hop_recv, hop_send, ex_recv, ex_send, ag_x, ag_y, ag_d, ag_o, ag_send):
     model = lax.axis_index("model")
     me = lax.axis_index("data")
@@ -144,11 +145,10 @@
 
 
     def exchange(buf, number):
-        @pl.loop(1, DEVICES)
-        def _(offset):
-            index = (linear + offset) % DEVICES
+        for flips in reversed(range(1, DEVICES)):
+            to_model, to_y, to_x, to_core = [at + (1 - 2 * at) * (flips >> bit & 1) for bit, at in zip((3, 2, 1, 0), (model, y, x, core))]
             pltpu.make_async_remote_copy(src_ref=buf.at[linear], dst_ref=buf.at[linear], send_sem=ex_send.at[number], recv_sem=ex_recv.at[number],
-                                         device_id={"model": index // DATA, "data": index % DATA}, device_id_type=MESH).start()
+                                         device_id={"model": to_model, "data": to_y * 4 + to_x * 2 + to_core}, device_id_type=MESH).start()
 
     def exchange_wait(buf, sem):
         others = buf.at[pl.ds(0, DEVICES - 1)]
@@ -161,6 +161,13 @@
         return total
 
     EX_WEIGHT, EX_GRAD, EX_FIRST = range(3)
+
+    def decay(state, factor):
+        @pl.loop(0, ROWS // 8 * PIECES)
+        def _(step):
+            rows = pl.ds(pl.multiple_of(step // PIECES * 8, 8), 8)
+            cols = pl.ds(pl.multiple_of(step % PIECES * PIECE, PIECE), PIECE)
+            state[rows, cols] = state[rows, cols] * factor
 
     def four(rows, cols_at, part):
         total = params[rows, pl.ds(pl.multiple_of(part * COLS + cols_at, PIECE), PIECE)].astype(F32)
@@ -194,6 +201,11 @@
             weight_buf[linear] = lax.fori_loop(0, ROWS // 8, weight_rows, jnp.zeros((8, 128), F32))
         if chunk == 2:
             exchange(weight_buf, EX_WEIGHT)
+            loads[1].wait()
+            decay(one, BETA_ONE)
+        if chunk == 3:
+            loads[2].wait()
+            decay(two, BETA_TWO)
 
     square = jnp.zeros((8, 128), F32)
     for chunk in range(RS_CHUNKS):
@@ -216,36 +228,38 @@
     for half in range(2):
         rows = pl.ds(half * HALF, HALF)
         pltpu.make_async_copy(relay.at[rows], relay.at[rows], hop_send.at[half]).wait()
-    for load in loads[1:]:
-        load.wait()
     exchange_wait(weight_buf, ex_recv.at[EX_WEIGHT])
     weight_norm = jnp.sqrt(tensor_total(gathered(weight_buf)))
     exchange_wait(norm_buf, ex_recv.at[EX_GRAD])
     grad_norm = jnp.sqrt(jnp.sum(gathered(norm_buf), axis=1, keepdims=True))
     clip = jnp.minimum(1.0, MAX_NORM / grad_norm)
 
-    def adam_row_sums(group):
-        rows = pl.ds(pl.multiple_of(group * 8, 8), 8)
-
-        def piece(i, total):
-            cols = pl.ds(pl.multiple_of(i * PIECE, PIECE), PIECE)
-            scaled = grad[rows, cols] * clip
-            new_one = BETA_ONE * one[rows, cols] + (1.0 - BETA_ONE) * scaled
-            new_two = BETA_TWO * two[rows, cols] + (1.0 - BETA_TWO) * (scaled * scaled)
-            one[rows, cols] = new_one
-            two[rows, cols] = new_two
-            direction = (new_one * (1.0 / CORR_ONE)) / (jnp.sqrt(new_two * (1.0 / CORR_TWO)) + EPSILON) + WEIGHT_DECAY * master[rows, cols]
-            relay[rows, cols] = direction
-            return total + fold_lanes(direction * direction)
-
-        total = lax.fori_loop(0, PIECES, piece, jnp.zeros((8, 128), F32))
-        return jnp.sum(total, axis=1, keepdims=True)
-
-    def adam_rows(group, tile):
-        return jnp.where(lane == group, adam_row_sums(group), tile)
-
-    def adam_first(group, tile):
-        return jnp.where(lane == 8 * group + sub, adam_row_sums(group), tile)
+    grad_one = (1.0 - BETA_ONE) * clip
+    grad_two = (1.0 - BETA_TWO) ** 0.5 * clip
+
+    def adam(start, stop):
+        @pl.loop(start, stop)
+        def _(group):
+            rows = pl.ds(pl.multiple_of(group * 8, 8), 8)
+            total = jnp.zeros((8, 128), F32)
+            for i in range(COLS // ADAM_PIECE):
+                cols = pl.ds(i * ADAM_PIECE, ADAM_PIECE)
+                mean = grad[rows, cols]
+                new_one = one[rows, cols] + grad_one * mean
+                scaled = grad_two * mean
+                new_two = two[rows, cols] + scaled * scaled
+                one[rows, cols] = new_one
+                two[rows, cols] = new_two
+                direction = new_one / (jnp.sqrt(new_two) * (CORR_ONE / CORR_TWO ** 0.5) + CORR_ONE * EPSILON) + WEIGHT_DECAY * master[rows, cols]
+                relay[rows, cols] = direction
+                total = total + fold_lanes(direction * direction)
+            part_buf[group] = total
+
+    def row_sums(start, stop, place):
+        tile = jnp.zeros((8, 128), F32)
+        for group in range(start, stop):
+            tile = jnp.where(lane == place(group), jnp.sum(part_buf[group], axis=1, keepdims=True), tile)
+        return tile
 
     def step_rates(number):
         if number == 0:
@@ -285,15 +299,17 @@
             remote(own, own, ag_send.at[2], ag_o, other).start()
 
     groups = [(start // 8, stop // 8) for start, stop in NORM_CHUNKS]
-    zero_tile = jnp.zeros((8, 128), F32)
-    first_buf[linear] = jnp.sum(lax.fori_loop(*groups[0], adam_first, zero_tile), axis=0, keepdims=True)
-    tile = lax.fori_loop(groups[1][0], groups[1][0] + 1, adam_rows, zero_tile)
+    adam(*groups[0])
+    first_buf[linear] = jnp.sum(row_sums(*groups[0], lambda group: 8 * group + sub), axis=0, keepdims=True)
+    adam(groups[1][0], groups[1][0] + 1)
     exchange(first_buf, EX_FIRST)
-    sq_buf[0, linear] = lax.fori_loop(groups[1][0] + 1, groups[1][1], adam_rows, tile)
-    tile = lax.fori_loop(groups[2][0], groups[2][0] + 1, adam_rows, zero_tile)
+    adam(groups[1][0] + 1, groups[1][1])
+    sq_buf[0, linear] = row_sums(*groups[1], lambda group: group)
+    adam(groups[2][0], groups[2][0] + 1)
     exchange(sq_buf.at[0], EX_FIRST + 1)
     update(0, step_rates(0))
-    sq_buf[1, linear] = lax.fori_loop(groups[2][0] + 1, groups[2][1], adam_rows, tile)
+    adam(groups[2][0] + 1, groups[2][1])
+    sq_buf[1, linear] = row_sums(*groups[2], lambda group: group)
     rates = step_rates(1)
     exchange(sq_buf.at[1], EX_FIRST + 2)
     update(1, rates)
@@ -369,6 +385,7 @@
                 pltpu.VMEM((DEVICES, 1, 128), F32),
                 pltpu.VMEM((DEVICES, 1, 128), F32),
                 pltpu.VMEM((2, DEVICES, 8, 128), F32),
+                pltpu.VMEM((ROWS // 8, 8, 128), F32),
                 dma((3,)),
                 dma((2, RS_CHUNKS)),
                 dma((2,)),

time: 343 us -> 340 us (level)
  no operation moved by 1% of the time
where the time goes in v3:
time: 340 us
  Pallas kernels  340 us (100%)
    pallas_call x1, Pallas kernels, device_step(): pl.pallas_call(kernel, name='lamb', out_shape=(pltpu.VMEM((ROWS, DATA * C...  324 us
    pallas_call x2, Pallas kernels, device_step(): pl.pallas_call(write_out, name='write_out', out_shape=[jax.ShapeDtypeStru...  15.2 us

profile of v3, /device:TPU:0, one launch (start us, length us, event | category | flops | bytes accessed | tf_op | source)
XLA Modules:
  0.0 340.2 jit_solution(10542125933922766250)
XLA Ops:
  0.6 324.3 %lamb.1 = (bf16[384,32768]{1,0:T(8,128)(2,1)S(1)}, f32[384,4096]{1,0:T(8,128)S(1)}, f32[384,4096]{1,0:T(8,128)S(1)}, f32[384,4096]{1,0:T(8,128)S(1)}) custom-call(bf16[1,384,32768]{2,1,0:T(8,128)(2,1)} %grad_ref.1, f32[384,4096]{1,0:T(8,128)} %master_ref.1, f32[384,4096]{1,0:T(8,128)} %one_ref.1, f32[384,4096]{1,0:T(8,128)} %two_ref.1), custom_call_target="tpu_custom_call" | custom-call | tf_op jit(solution)/shard_map/lamb/pallas_call | solution.py:375
  325.0 8.6 %write_out.2 = bf16[384,32768]{1,0:T(8,128)(2,1)} custom-call(bf16[384,32768]{1,0:T(8,128)(2,1)S(1)} %get-tuple-element.11.refs_0_), custom_call_target="tpu_custom_call" | custom-call | tf_op jit(solution)/shard_map/write_out/pallas_call | solution.py:406
  333.6 6.6 %write_out.3 = (f32[384,4096]{1,0:T(8,128)}, f32[384,4096]{1,0:T(8,128)}, f32[384,4096]{1,0:T(8,128)}) custom-call(f32[384,4096]{1,0:T(8,128)S(1)} %get-tuple-element.12.refs_0_, f32[384,4096]{1,0:T(8,128)S(1)} %get-tuple-element.13.refs_1_, f32[384,4096]{1,0:T(8,128)S(1)} %get-tuple-element.14.refs_2_), custom_call_target="tpu_custom_call" | custom-call | tf_op jit(solution)/shard_map/write_out/pallas_call | solution.py:406

commit v4 on v3

--- a/solution.py
+++ b/solution.py
@@ -1,3 +1,5 @@
+import functools
+
 import jax
 import jax.numpy as jnp
 from jax import lax
@@ -27,11 +29,11 @@
 RS_SIZES = (48, 48, 48, 32, 16)
 RS_CHUNKS = len(RS_SIZES)
 RS_STARTS = tuple(sum(RS_SIZES[:i]) for i in range(RS_CHUNKS))
-AG_SIZES = (32,) * 10 + (16,) * 4
+AG_SIZES = (16,) * 2 + (32,) * 9 + (16,) * 4
+AG_FAR_BY_Y = (1, 0) + (1, 0) * 4 + (1,) + (0, 0, 1, 0)
 AG_CHUNKS = len(AG_SIZES)
 AG_STARTS = tuple(sum(AG_SIZES[:i]) for i in range(AG_CHUNKS))
 NORM_CHUNKS = ((0, 32), (32, 288), (288, 384))
-OUT_PARTS = 4
 
 MESH = pl.DeviceIdType.MESH
 F32 = jnp.float32
@@ -73,7 +75,7 @@
 
 
 def kernel(grad_ref, master_ref, one_ref, two_ref, params, master, one, two, relay, grad, weight_buf, norm_buf, first_buf, sq_buf, part_buf,
-           load_sem, rs_recv, rs_send, hop_recv, hop_send, ex_recv, ex_send, ag_x, ag_y, ag_d, ag_o, ag_send):
+           load_sem, rs_recv, rs_send, hop_recv, hop_send, ex_recv, ex_send, ag_x, ag_y, ag_d, ag_o, ag_send, plane_sem):
     model = lax.axis_index("model")
     me = lax.axis_index("data")
     linear = model * DATA + me
@@ -99,12 +101,10 @@
 
     barrier = pltpu.get_barrier_semaphore()
 
-    @pl.loop(1, DEVICES)
-    def _(offset):
-        index = (linear + offset) % DEVICES
-        pl.semaphore_signal(barrier, inc=1, device_id={"model": index // DATA, "data": index % DATA}, device_id_type=MESH)
-
-    pl.semaphore_wait(barrier, DEVICES - 1)
+    mirror = {"model": 1 - model, "data": me}
+    for neighbour in (peer(near_x), peer(near_x + to_core), peer(near_y), peer(near_y + to_core), mirror, peer(other)):
+        pl.semaphore_signal(barrier, inc=1, device_id=neighbour, device_id_type=MESH)
+    pl.semaphore_wait(barrier, 6)
 
     def remote(source, target, send, recv, index):
         return pltpu.make_async_remote_copy(src_ref=source, dst_ref=target, send_sem=send, recv_sem=recv,
@@ -192,6 +192,8 @@
                 relay[tile_rows, pl.ds(pl.multiple_of(cols_at, PIECE), PIECE)] = four(tile_rows, cols_at, 1)
 
             hop(half, chunk).start()
+        if chunk == 0:
+            pl.semaphore_signal(plane_sem, inc=1, device_id=mirror, device_id_type=MESH)
         if chunk + 1 < RS_CHUNKS:
             load_own(chunk + 1)
         if chunk < 3:
@@ -200,6 +202,7 @@
             loads[0].wait()
             weight_buf[linear] = lax.fori_loop(0, ROWS // 8, weight_rows, jnp.zeros((8, 128), F32))
         if chunk == 2:
+            pl.semaphore_wait(plane_sem, 1)
             exchange(weight_buf, EX_WEIGHT)
             loads[1].wait()
             decay(one, BETA_ONE)
@@ -323,11 +326,11 @@
     for chunk in range(AG_CHUNKS):
         rows = ag_rows(chunk)
         view = arrived(ag_x.at[chunk], near_x, rows)
-        if chunk % 2 == 0:
+        if AG_FAR_BY_Y[chunk]:
             remote(view, view, ag_send.at[1], ag_d.at[chunk], near_y).start()
         remote(view, view, ag_send.at[2], ag_o, other).start()
         view = arrived(ag_y.at[chunk], near_y, rows)
-        if chunk % 2 == 1:
+        if not AG_FAR_BY_Y[chunk]:
             remote(view, view, ag_send.at[0], ag_d.at[chunk], near_x).start()
         remote(view, view, ag_send.at[2], ag_o, other).start()
 
@@ -352,16 +355,16 @@
         exchange_wait(sq_buf.at[number], ex_send.at[EX_FIRST + 1 + number])
 
 
-def write_out(*refs):
+def write_out(parts, *refs):
     count = len(refs) // 2
     sem = refs[-1]
     copies = []
-    for source, target in zip(refs[:count], refs[count:-1]):
-        for part in range(OUT_PARTS):
-            rows = pl.ds(part * (ROWS // OUT_PARTS), ROWS // OUT_PARTS)
+    for part in range(parts):
+        rows = pl.ds(part * (ROWS // parts), ROWS // parts)
+        for source, target in zip(refs[:count], refs[count:-1]):
             copies.append(pltpu.make_async_copy(source.at[rows], target.at[rows], sem.at[len(copies)]))
-    for copy in copies:
-        copy.start()
+    for number, copy in enumerate(copies):
+        copy.start(priority=number % 2)
     for copy in copies:
         copy.wait()
 
@@ -398,18 +401,19 @@
                 dma((AG_CHUNKS,)),
                 dma,
                 dma((3,)),
+                pltpu.SemaphoreType.REGULAR,
             ],
             compiler_params=pltpu.CompilerParams(collective_id=0, has_side_effects=True, vmem_limit_bytes=16 << 20),
         )(local_grads, master, moment_one, moment_two)
         written = []
-        for group in (results[:1], results[1:]):
+        for group, parts in ((results[:1], 12), (results[1:], 4)):
             written += pl.pallas_call(
-                write_out,
+                functools.partial(write_out, parts),
                 name="write_out",
                 out_shape=[jax.ShapeDtypeStruct(value.shape, value.dtype) for value in group],
                 in_specs=[vmem_spec] * len(group),
                 out_specs=[any_spec] * len(group),
-                scratch_shapes=[dma((len(group) * OUT_PARTS,))],
+                scratch_shapes=[dma((len(group) * parts,))],
                 compiler_params=pltpu.CompilerParams(vmem_limit_bytes=1 << 20),
             )(*group)
         return tuple(written)

time: 340 us -> 339 us (level)
  no operation moved by 1% of the time
where the time goes in v4:
time: 339 us
  Pallas kernels  338 us (100%)
    pallas_call x1, Pallas kernels, device_step(): pl.pallas_call(kernel, name='lamb', out_shape=(pltpu.VMEM((ROWS, DATA * C...  323 us
    pallas_call x2, Pallas kernels, device_step(): pl.pallas_call(functools.partial(write_out, parts), name='write_out', out...  15.1 us

profile of v4, /device:TPU:0, one launch (start us, length us, event | category | flops | bytes accessed | tf_op | source)
XLA Modules:
  0.0 338.6 jit_solution(1300143399926597981)
XLA Ops:
  0.6 322.9 %lamb.1 = (bf16[384,32768]{1,0:T(8,128)(2,1)S(1)}, f32[384,4096]{1,0:T(8,128)S(1)}, f32[384,4096]{1,0:T(8,128)S(1)}, f32[384,4096]{1,0:T(8,128)S(1)}) custom-call(bf16[1,384,32768]{2,1,0:T(8,128)(2,1)} %grad_ref.1, f32[384,4096]{1,0:T(8,128)} %master_ref.1, f32[384,4096]{1,0:T(8,128)} %one_ref.1, f32[384,4096]{1,0:T(8,128)} %two_ref.1), custom_call_target="tpu_custom_call" | custom-call | tf_op jit(solution)/shard_map/lamb/pallas_call | solution.py:378
  323.5 8.5 %write_out.2 = bf16[384,32768]{1,0:T(8,128)(2,1)} custom-call(bf16[384,32768]{1,0:T(8,128)(2,1)S(1)} %get-tuple-element.11.refs_0_), custom_call_target="tpu_custom_call" | custom-call | tf_op jit(solution)/shard_map/write_out/pallas_call | solution.py:410
  332.0 6.6 %write_out.3 = (f32[384,4096]{1,0:T(8,128)}, f32[384,4096]{1,0:T(8,128)}, f32[384,4096]{1,0:T(8,128)}) custom-call(f32[384,4096]{1,0:T(8,128)S(1)} %get-tuple-element.12.refs_0_, f32[384,4096]{1,0:T(8,128)S(1)} %get-tuple-element.13.refs_1_, f32[384,4096]{1,0:T(8,128)S(1)} %get-tuple-element.14.refs_2_), custom_call_target="tpu_custom_call" | custom-call | tf_op jit(solution)/shard_map/write_out/pallas_call | solution.py:410

commit v5 on v4

--- a/solution.py
+++ b/solution.py
@@ -1,5 +1,3 @@
-import functools
-
 import jax
 import jax.numpy as jnp
 from jax import lax
@@ -25,15 +23,17 @@
 PIECE = 1024
 PIECES = COLS // PIECE
 ADAM_PIECE = 1024
+OUT_PARTS = 6
+VMEM_LIMIT = 16 << 20
 
 RS_SIZES = (48, 48, 48, 32, 16)
 RS_CHUNKS = len(RS_SIZES)
 RS_STARTS = tuple(sum(RS_SIZES[:i]) for i in range(RS_CHUNKS))
-AG_SIZES = (16,) * 2 + (32,) * 9 + (16,) * 4
-AG_FAR_BY_Y = (1, 0) + (1, 0) * 4 + (1,) + (0, 0, 1, 0)
+AG_SIZES = (16,) + (32,) * 10 + (16,) * 3
+AG_FAR_BY_Y = (1,) + (0, 1) * 5 + (0, 1, 0)
 AG_CHUNKS = len(AG_SIZES)
 AG_STARTS = tuple(sum(AG_SIZES[:i]) for i in range(AG_CHUNKS))
-NORM_CHUNKS = ((0, 32), (32, 288), (288, 384))
+NORM_CHUNKS = ((0, 16), (16, 208), (208, 384))
 
 MESH = pl.DeviceIdType.MESH
 F32 = jnp.float32
@@ -355,12 +355,12 @@
         exchange_wait(sq_buf.at[number], ex_send.at[EX_FIRST + 1 + number])
 
 
-def write_out(parts, *refs):
+def write_out(*refs):
     count = len(refs) // 2
     sem = refs[-1]
     copies = []
-    for part in range(parts):
-        rows = pl.ds(part * (ROWS // parts), ROWS // parts)
+    for part in range(OUT_PARTS):
+        rows = pl.ds(part * (ROWS // OUT_PARTS), ROWS // OUT_PARTS)
         for source, target in zip(refs[:count], refs[count:-1]):
             copies.append(pltpu.make_async_copy(source.at[rows], target.at[rows], sem.at[len(copies)]))
     for number, copy in enumerate(copies):
@@ -403,20 +403,18 @@
                 dma((3,)),
                 pltpu.SemaphoreType.REGULAR,
             ],
-            compiler_params=pltpu.CompilerParams(collective_id=0, has_side_effects=True, vmem_limit_bytes=16 << 20),
+            compiler_params=pltpu.CompilerParams(collective_id=0, has_side_effects=True, vmem_limit_bytes=VMEM_LIMIT),
         )(local_grads, master, moment_one, moment_two)
-        written = []
-        for group, parts in ((results[:1], 12), (results[1:], 4)):
-            written += pl.pallas_call(
-                functools.partial(write_out, parts),
-                name="write_out",
-                out_shape=[jax.ShapeDtypeStruct(value.shape, value.dtype) for value in group],
-                in_specs=[vmem_spec] * len(group),
-                out_specs=[any_spec] * len(group),
-                scratch_shapes=[dma((len(group) * parts,))],
-                compiler_params=pltpu.CompilerParams(vmem_limit_bytes=1 << 20),
-            )(*group)
-        return tuple(written)
+        results = [pltpu.with_memory_space_constraint(value, pltpu.VMEM) for value in results]
+        return tuple(pl.pallas_call(
+            write_out,
+            name="write_out",
+            out_shape=[jax.ShapeDtypeStruct(value.shape, value.dtype) for value in results],
+            in_specs=[vmem_spec] * 4,
+            out_specs=[any_spec] * 4,
+            scratch_shapes=[dma((4 * OUT_PARTS,))],
+            compiler_params=pltpu.CompilerParams(vmem_limit_bytes=VMEM_LIMIT),
+        )(*results))
 
     state_spec = P(None, ('model', 'data'))
     return jax.shard_map(device_step, mesh=mesh, in_specs=(P('data', None, 'model'), state_spec, state_spec, state_spec), out_specs=(P(None, 'model'), state_spec, state_spec, state_spec), check_vma=False)

time: 339 us -> 337 us (level)
    pallas_call x2 -> x1, Pallas kernels: 15.1 us -> 14.2 us  [device_step(): pl.pallas_call(write_out, name='write_out', out_shape=[jax.ShapeDtypeStru...]
where the time goes in v5:
time: 337 us
  Pallas kernels  337 us (100%)
    pallas_call x1, Pallas kernels, device_step(): pl.pallas_call(kernel, name='lamb', out_shape=(pltpu.VMEM((ROWS, DATA * C...  322 us
    pallas_call x1, Pallas kernels, device_step(): pl.pallas_call(write_out, name='write_out', out_shape=[jax.ShapeDtypeStru...  14.2 us

profile of v5, /device:TPU:0, one launch (start us, length us, event | category | flops | bytes accessed | tf_op | source)
XLA Modules:
  0.0 337.2 jit_solution(5249306503140585971)
XLA Ops:
  0.6 322.3 %lamb.1 = (bf16[384,32768]{1,0:T(8,128)(2,1)S(1)}, f32[384,4096]{1,0:T(8,128)S(1)}, f32[384,4096]{1,0:T(8,128)S(1)}, f32[384,4096]{1,0:T(8,128)S(1)}) custom-call(bf16[1,384,32768]{2,1,0:T(8,128)(2,1)} %grad_ref.1, f32[384,4096]{1,0:T(8,128)} %master_ref.1, f32[384,4096]{1,0:T(8,128)} %one_ref.1, f32[384,4096]{1,0:T(8,128)} %two_ref.1), custom_call_target="tpu_custom_call" | custom-call | tf_op jit(solution)/shard_map/lamb/pallas_call | solution.py:378
  322.9 14.2 %write_out.1 = (bf16[384,32768]{1,0:T(8,128)(2,1)}, f32[384,4096]{1,0:T(8,128)}, f32[384,4096]{1,0:T(8,128)}, f32[384,4096]{1,0:T(8,128)}) custom-call(bf16[384,32768]{1,0:T(8,128)(2,1)S(1)} %get-tuple-element.8.refs_0_, f32[384,4096]{1,0:T(8,128)S(1)} %get-tuple-element.9.refs_1_, f32[384,4096]{1,0:T(8,128)S(1)} %get-tuple-element.10.refs_2_, ...), custom_call_target="tpu_custom_call" | custom-call | tf_op jit(solution)/shard_map/write_out/pallas_call | solution.py:409

commit v6 on v5

--- a/solution.py
+++ b/solution.py
@@ -23,6 +23,8 @@
 PIECE = 1024
 PIECES = COLS // PIECE
 ADAM_PIECE = 1024
+LEAD = 16
+EARLY = 2048
 OUT_PARTS = 6
 VMEM_LIMIT = 16 << 20
 
@@ -74,8 +76,9 @@
     return tile
 
 
-def kernel(grad_ref, master_ref, one_ref, two_ref, params, master, one, two, relay, grad, weight_buf, norm_buf, first_buf, sq_buf, part_buf,
-           load_sem, rs_recv, rs_send, hop_recv, hop_send, ex_recv, ex_send, ag_x, ag_y, ag_d, ag_o, ag_send, plane_sem):
+def kernel(grad_ref, master_ref, one_ref, two_ref, params, master, one, two, relay, grad, weight_buf, norm_buf, first_buf, sq_buf, part_buf, lead, early,
+           load_sem, rs_recv, rs_send, hop_recv, hop_send, ex_recv, ex_send, ag_x, ag_y, ag_d, ag_o, ag_send, plane_sem,
+           lead_sem, early_recv, early_send):
     model = lax.axis_index("model")
     me = lax.axis_index("data")
     linear = model * DATA + me
@@ -99,6 +102,10 @@
     def rows_of(half, chunk):
         return pl.ds(half * HALF + RS_STARTS[chunk], RS_SIZES[chunk])
 
+    leads = [pltpu.make_async_copy(grad_ref.at[0, pl.ds(half * HALF, LEAD), block(first[half])], lead.at[half], lead_sem.at[half]) for half in range(2)]
+    for copy in leads:
+        copy.start()
+
     barrier = pltpu.get_barrier_semaphore()
 
     mirror = {"model": 1 - model, "data": me}
@@ -118,7 +125,13 @@
             for turn in range(2):
                 shift = turn * to_core
                 for part, owner in enumerate((first[half] + shift, diag + shift)):
-                    remote(grad_ref.at[0, rows, block(owner)], params.at[rows, pl.ds((4 + 2 * turn + part) * COLS, COLS)], send, recv, first[half] + shift).start()
+                    place = pl.ds((4 + 2 * turn + part) * COLS, COLS)
+                    sent = rows
+                    if (chunk, turn, part) == (0, 0, 0):
+                        leads[half].wait()
+                        remote(lead.at[half], params.at[pl.ds(half * HALF, LEAD), place], send, recv, first[half]).start()
+                        sent = pl.ds(half * HALF + LEAD, RS_SIZES[0] - LEAD)
+                    remote(grad_ref.at[0, sent, block(owner)], params.at[sent, place], send, recv, first[half] + shift).start()
             for part, owner in enumerate((other, second[half] + to_core)):
                 remote(grad_ref.at[0, rows, block(owner)], params.at[rows, pl.ds((2 + part) * COLS, COLS)], send, recv, other).start()
 
@@ -227,7 +240,17 @@
             square = lax.fori_loop(0, RS_SIZES[chunk] // 16 * PIECES, finish, square)
 
     norm_buf[linear] = jnp.sum(square, axis=0, keepdims=True)
+    def send_early(kind, source):
+        for side, near in enumerate((near_x, near_y)):
+            remote(source.at[pl.ds(0, 16), pl.ds(0, EARLY)], early.at[kind, side], early_send.at[kind, side], early_recv.at[kind, side], near).start()
+
+    def early_wait(sem, kind):
+        for side in range(2):
+            view = early.at[kind, side]
+            pltpu.make_async_copy(view, view, sem.at[kind, side]).wait()
+
     exchange(norm_buf, EX_GRAD)
+    send_early(0, master)
     for half in range(2):
         rows = pl.ds(half * HALF, HALF)
         pltpu.make_async_copy(relay.at[rows], relay.at[rows], hop_send.at[half]).wait()
@@ -276,6 +299,12 @@
     def ag_rows(chunk):
         return pl.ds(AG_STARTS[chunk], AG_SIZES[chunk])
 
+    def rate_column(rates, group):
+        return jnp.concatenate([jnp.sum(jnp.where(lane == group + i, rates, 0.0), axis=1, keepdims=True) for i in range(2)], axis=0)
+
+    def late_part(chunk, source):
+        return params.at[ag_rows(chunk), pl.ds(pl.multiple_of(source * COLS + EARLY, EARLY), COLS - EARLY)]
+
     def update(number, rates):
         start, stop = NORM_CHUNKS[number]
         for chunk in range(AG_CHUNKS):
@@ -286,7 +315,7 @@
             def _(tile):
                 group = AG_STARTS[chunk] // 8 + 2 * tile
                 rows = pl.ds(pl.multiple_of(AG_STARTS[chunk] + tile * 16, 16), 16)
-                rate = jnp.concatenate([jnp.sum(jnp.where(lane == group + i, rates, 0.0), axis=1, keepdims=True) for i in range(2)], axis=0)
+                rate = rate_column(rates, group)
 
                 @pl.loop(0, PIECES)
                 def _(i):
@@ -297,8 +326,9 @@
 
             rows = ag_rows(chunk)
             own = params.at[rows, block(me)]
-            remote(own, own, ag_send.at[0], ag_x.at[chunk], near_x).start()
-            remote(own, own, ag_send.at[1], ag_y.at[chunk], near_y).start()
+            near = late_part(chunk, me) if chunk == 0 else own
+            remote(near, near, ag_send.at[0], ag_x.at[chunk], near_x).start()
+            remote(near, near, ag_send.at[1], ag_y.at[chunk], near_y).start()
             remote(own, own, ag_send.at[2], ag_o, other).start()
 
     groups = [(start // 8, stop // 8) for start, stop in NORM_CHUNKS]
@@ -306,45 +336,58 @@
     first_buf[linear] = jnp.sum(row_sums(*groups[0], lambda group: 8 * group + sub), axis=0, keepdims=True)
     adam(groups[1][0], groups[1][0] + 1)
     exchange(first_buf, EX_FIRST)
+    send_early(1, relay)
     adam(groups[1][0] + 1, groups[1][1])
     sq_buf[0, linear] = row_sums(*groups[1], lambda group: group)
     adam(groups[2][0], groups[2][0] + 1)
     exchange(sq_buf.at[0], EX_FIRST + 1)
-    update(0, step_rates(0))
+    first_rates = step_rates(0)
+    early_wait(early_send, 0)
+    update(0, first_rates)
     adam(groups[2][0] + 1, groups[2][1])
     sq_buf[1, linear] = row_sums(*groups[2], lambda group: group)
     rates = step_rates(1)
     exchange(sq_buf.at[1], EX_FIRST + 2)
     update(1, rates)
+    rate = rate_column(first_rates, 0)
+    for kind in range(2):
+        early_wait(early_recv, kind)
+    for side, near in enumerate((near_x, near_y)):
+        @pl.loop(0, EARLY // PIECE)
+        def _(i):
+            cols = pl.ds(pl.multiple_of(i * PIECE, PIECE), PIECE)
+            value = early[0, side, :, cols] - rate * early[1, side, :, cols]
+            params[pl.ds(0, 16), pl.ds(pl.multiple_of(near * COLS + i * PIECE, PIECE), PIECE)] = value.astype(BF16)
+
     update(2, step_rates(2))
 
-    def arrived(sem, source, rows):
-        view = params.at[rows, block(source)]
+    def arrived(sem, source, chunk, early_part=False):
+        view = late_part(chunk, source) if early_part else params.at[ag_rows(chunk), block(source)]
         pltpu.make_async_copy(view, view, sem).wait()
-        return view
+        return params.at[ag_rows(chunk), block(source)]
 
     for chunk in range(AG_CHUNKS):
-        rows = ag_rows(chunk)
-        view = arrived(ag_x.at[chunk], near_x, rows)
+        view = arrived(ag_x.at[chunk], near_x, chunk, chunk == 0)
         if AG_FAR_BY_Y[chunk]:
             remote(view, view, ag_send.at[1], ag_d.at[chunk], near_y).start()
         remote(view, view, ag_send.at[2], ag_o, other).start()
-        view = arrived(ag_y.at[chunk], near_y, rows)
+        view = arrived(ag_y.at[chunk], near_y, chunk, chunk == 0)
         if not AG_FAR_BY_Y[chunk]:
             remote(view, view, ag_send.at[0], ag_d.at[chunk], near_x).start()
         remote(view, view, ag_send.at[2], ag_o, other).start()
 
     for chunk in range(AG_CHUNKS):
-        view = arrived(ag_d.at[chunk], diag, ag_rows(chunk))
+        view = arrived(ag_d.at[chunk], diag, chunk)
         remote(view, view, ag_send.at[2], ag_o, other).start()
 
     half_cols = params.at[:, pl.ds(0, DATA // 2 * COLS)]
     pltpu.make_async_copy(half_cols, half_cols, ag_o).wait()
     pltpu.make_async_copy(half_cols, half_cols, ag_send.at[2]).wait()
     for direction in range(2):
-        for part in (pl.ds(0, ROWS), pl.ds(0, HALF)):
-            view = params.at[part, pl.ds(0, COLS)]
+        for rows, cols in ((ROWS - 16, COLS), (16, COLS - EARLY), (HALF, COLS)):
+            view = params.at[pl.ds(0, rows), pl.ds(0, cols)]
             pltpu.make_async_copy(view, view, ag_send.at[direction]).wait()
+    early_wait(early_send, 1)
     for half in range(2):
         view = params.at[pl.ds(0, HALF), pl.ds(0, 6 * COLS)]
         pltpu.make_async_copy(view, view, rs_send.at[half]).wait()
@@ -389,6 +432,8 @@
                 pltpu.VMEM((DEVICES, 1, 128), F32),
                 pltpu.VMEM((2, DEVICES, 8, 128), F32),
                 pltpu.VMEM((ROWS // 8, 8, 128), F32),
+                pltpu.VMEM((2, LEAD, COLS), BF16),
+                pltpu.VMEM((2, 2, 16, EARLY), F32),
                 dma((3,)),
                 dma((2, RS_CHUNKS)),
                 dma((2,)),
@@ -402,6 +447,9 @@
                 dma,
                 dma((3,)),
                 pltpu.SemaphoreType.REGULAR,
+                dma((2,)),
+                dma((2, 2)),
+                dma((2, 2)),
             ],
             compiler_params=pltpu.CompilerParams(collective_id=0, has_side_effects=True, vmem_limit_bytes=VMEM_LIMIT),
         )(local_grads, master, moment_one, moment_two)

time: 337 us -> 337 us (level)
  no operation moved by 1% of the time
where the time goes in v6:
time: 337 us
  Pallas kernels  337 us (100%)
    pallas_call x1, Pallas kernels, device_step(): pl.pallas_call(kernel, name='lamb', out_shape=(pltpu.VMEM((ROWS, DATA * C...  322 us
    pallas_call x1, Pallas kernels, device_step(): pl.pallas_call(write_out, name='write_out', out_shape=[jax.ShapeDtypeStru...  14.2 us

profile of v6, /device:TPU:0, one launch (start us, length us, event | category | flops | bytes accessed | tf_op | source)
XLA Modules:
  0.0 337.3 jit_solution(4815191464091111460)
XLA Ops:
  0.6 322.5 %lamb.1 = (bf16[384,32768]{1,0:T(8,128)(2,1)S(1)}, f32[384,4096]{1,0:T(8,128)S(1)}, f32[384,4096]{1,0:T(8,128)S(1)}, f32[384,4096]{1,0:T(8,128)S(1)}) custom-call(bf16[1,384,32768]{2,1,0:T(8,128)(2,1)} %grad_ref.1, f32[384,4096]{1,0:T(8,128)} %master_ref.1, f32[384,4096]{1,0:T(8,128)} %one_ref.1, f32[384,4096]{1,0:T(8,128)} %two_ref.1), custom_call_target="tpu_custom_call" | custom-call | tf_op jit(solution)/shard_map/lamb/pallas_call | solution.py:421
  323.1 14.2 %write_out.1 = (bf16[384,32768]{1,0:T(8,128)(2,1)}, f32[384,4096]{1,0:T(8,128)}, f32[384,4096]{1,0:T(8,128)}, f32[384,4096]{1,0:T(8,128)}) custom-call(bf16[384,32768]{1,0:T(8,128)(2,1)S(1)} %get-tuple-element.8.refs_0_, f32[384,4096]{1,0:T(8,128)S(1)} %get-tuple-element.9.refs_1_, f32[384,4096]{1,0:T(8,128)S(1)} %get-tuple-element.10.refs_2_, ...), custom_call_target="tpu_custom_call" | custom-call | tf_op jit(solution)/shard_map/write_out/pallas_call | solution.py:457

commit v7 on v5

--- a/solution.py
+++ b/solution.py
@@ -23,6 +23,7 @@
 PIECE = 1024
 PIECES = COLS // PIECE
 ADAM_PIECE = 1024
+LEAD = 16
 OUT_PARTS = 6
 VMEM_LIMIT = 16 << 20
 
@@ -74,8 +75,8 @@
     return tile
 
 
-def kernel(grad_ref, master_ref, one_ref, two_ref, params, master, one, two, relay, grad, weight_buf, norm_buf, first_buf, sq_buf, part_buf,
-           load_sem, rs_recv, rs_send, hop_recv, hop_send, ex_recv, ex_send, ag_x, ag_y, ag_d, ag_o, ag_send, plane_sem):
+def kernel(grad_ref, master_ref, one_ref, two_ref, params, master, one, two, relay, grad, weight_buf, norm_buf, first_buf, sq_buf, part_buf, lead,
+           load_sem, rs_recv, rs_send, hop_recv, hop_send, ex_recv, ex_send, ag_x, ag_y, ag_d, ag_o, ag_send, plane_sem, lead_sem):
     model = lax.axis_index("model")
     me = lax.axis_index("data")
     linear = model * DATA + me
@@ -99,6 +100,10 @@
     def rows_of(half, chunk):
         return pl.ds(half * HALF + RS_STARTS[chunk], RS_SIZES[chunk])
 
+    leads = [pltpu.make_async_copy(grad_ref.at[0, pl.ds(half * HALF, LEAD), block(first[half])], lead.at[half], lead_sem.at[half]) for half in range(2)]
+    for copy in leads:
+        copy.start()
+
     barrier = pltpu.get_barrier_semaphore()
 
     mirror = {"model": 1 - model, "data": me}
@@ -118,7 +123,13 @@
             for turn in range(2):
                 shift = turn * to_core
                 for part, owner in enumerate((first[half] + shift, diag + shift)):
-                    remote(grad_ref.at[0, rows, block(owner)], params.at[rows, pl.ds((4 + 2 * turn + part) * COLS, COLS)], send, recv, first[half] + shift).start()
+                    place = pl.ds((4 + 2 * turn + part) * COLS, COLS)
+                    sent = rows
+                    if (chunk, turn, part) == (0, 0, 0):
+                        leads[half].wait()
+                        remote(lead.at[half], params.at[pl.ds(half * HALF, LEAD), place], send, recv, first[half]).start()
+                        sent = pl.ds(half * HALF + LEAD, RS_SIZES[0] - LEAD)
+                    remote(grad_ref.at[0, sent, block(owner)], params.at[sent, place], send, recv, first[half] + shift).start()
             for part, owner in enumerate((other, second[half] + to_core)):
                 remote(grad_ref.at[0, rows, block(owner)], params.at[rows, pl.ds((2 + part) * COLS, COLS)], send, recv, other).start()
 
@@ -389,6 +400,7 @@
                 pltpu.VMEM((DEVICES, 1, 128), F32),
                 pltpu.VMEM((2, DEVICES, 8, 128), F32),
                 pltpu.VMEM((ROWS // 8, 8, 128), F32),
+                pltpu.VMEM((2, LEAD, COLS), BF16),
                 dma((3,)),
                 dma((2, RS_CHUNKS)),
                 dma((2,)),
@@ -402,6 +414,7 @@
                 dma,
                 dma((3,)),
                 pltpu.SemaphoreType.REGULAR,
+                dma((2,)),
             ],
             compiler_params=pltpu.CompilerParams(collective_id=0, has_side_effects=True, vmem_limit_bytes=VMEM_LIMIT),
         )(local_grads, master, moment_one, moment_two)

time: 337 us -> 337 us (level)
  no operation moved by 1% of the time
where the time goes in v7:
time: 337 us
  Pallas kernels  337 us (100%)
    pallas_call x1, Pallas kernels, device_step(): pl.pallas_call(kernel, name='lamb', out_shape=(pltpu.VMEM((ROWS, DATA * C...  322 us
    pallas_call x1, Pallas kernels, device_step(): pl.pallas_call(write_out, name='write_out', out_shape=[jax.ShapeDtypeStru...  14.2 us

profile of v7, /device:TPU:0, one launch (start us, length us, event | category | flops | bytes accessed | tf_op | source)
XLA Modules:
  0.0 337.2 jit_solution(3499079833068966148)
XLA Ops:
  0.6 322.3 %lamb.1 = (bf16[384,32768]{1,0:T(8,128)(2,1)S(1)}, f32[384,4096]{1,0:T(8,128)S(1)}, f32[384,4096]{1,0:T(8,128)S(1)}, f32[384,4096]{1,0:T(8,128)S(1)}) custom-call(bf16[1,384,32768]{2,1,0:T(8,128)(2,1)} %grad_ref.1, f32[384,4096]{1,0:T(8,128)} %master_ref.1, f32[384,4096]{1,0:T(8,128)} %one_ref.1, f32[384,4096]{1,0:T(8,128)} %two_ref.1), custom_call_target="tpu_custom_call" | custom-call | tf_op jit(solution)/shard_map/lamb/pallas_call | solution.py:389
  323.0 14.2 %write_out.1 = (bf16[384,32768]{1,0:T(8,128)(2,1)}, f32[384,4096]{1,0:T(8,128)}, f32[384,4096]{1,0:T(8,128)}, f32[384,4096]{1,0:T(8,128)}) custom-call(bf16[384,32768]{1,0:T(8,128)(2,1)S(1)} %get-tuple-element.8.refs_0_, f32[384,4096]{1,0:T(8,128)S(1)} %get-tuple-element.9.refs_1_, f32[384,4096]{1,0:T(8,128)S(1)} %get-tuple-element.10.refs_2_, ...), custom_call_target="tpu_custom_call" | custom-call | tf_op jit(solution)/shard_map/write_out/pallas_call | solution.py:422

commit v8 on v5

--- a/solution.py
+++ b/solution.py
@@ -119,14 +119,14 @@
                 shift = turn * to_core
                 for part, owner in enumerate((first[half] + shift, diag + shift)):
                     remote(grad_ref.at[0, rows, block(owner)], params.at[rows, pl.ds((4 + 2 * turn + part) * COLS, COLS)], send, recv, first[half] + shift).start()
-            for part, owner in enumerate((other, second[half] + to_core)):
-                remote(grad_ref.at[0, rows, block(owner)], params.at[rows, pl.ds((2 + part) * COLS, COLS)], send, recv, other).start()
 
     def load_own(chunk):
         for half in range(2):
             rows = rows_of(half, chunk)
             for part, owner in enumerate((me, second[half])):
                 pltpu.make_async_copy(grad_ref.at[0, rows, block(owner)], params.at[rows, pl.ds(part * COLS, COLS)], rs_recv.at[half, chunk]).start()
+            for part, owner in enumerate((other, second[half] + to_core)):
+                remote(grad_ref.at[0, rows, block(owner)], params.at[rows, pl.ds((2 + part) * COLS, COLS)], rs_send.at[half], rs_recv.at[half, chunk], other).start()
 
     load_own(0)
 

time: 337 us -> 337 us (level)
  no operation moved by 1% of the time
where the time goes in v8:
time: 337 us
  Pallas kernels  337 us (100%)
    pallas_call x1, Pallas kernels, device_step(): pl.pallas_call(kernel, name='lamb', out_shape=(pltpu.VMEM((ROWS, DATA * C...  322 us
    pallas_call x1, Pallas kernels, device_step(): pl.pallas_call(write_out, name='write_out', out_shape=[jax.ShapeDtypeStru...  14.2 us

profile of v8, /device:TPU:0, one launch (start us, length us, event | category | flops | bytes accessed | tf_op | source)
XLA Modules:
  0.0 337.2 jit_solution(8703032123335479486)
XLA Ops:
  0.6 322.3 %lamb.1 = (bf16[384,32768]{1,0:T(8,128)(2,1)S(1)}, f32[384,4096]{1,0:T(8,128)S(1)}, f32[384,4096]{1,0:T(8,128)S(1)}, f32[384,4096]{1,0:T(8,128)S(1)}) custom-call(bf16[1,384,32768]{2,1,0:T(8,128)(2,1)} %grad_ref.1, f32[384,4096]{1,0:T(8,128)} %master_ref.1, f32[384,4096]{1,0:T(8,128)} %one_ref.1, f32[384,4096]{1,0:T(8,128)} %two_ref.1), custom_call_target="tpu_custom_call" | custom-call | tf_op jit(solution)/shard_map/lamb/pallas_call | solution.py:378
  322.9 14.2 %write_out.1 = (bf16[384,32768]{1,0:T(8,128)(2,1)}, f32[384,4096]{1,0:T(8,128)}, f32[384,4096]{1,0:T(8,128)}, f32[384,4096]{1,0:T(8,128)}) custom-call(bf16[384,32768]{1,0:T(8,128)(2,1)S(1)} %get-tuple-element.8.refs_0_, f32[384,4096]{1,0:T(8,128)S(1)} %get-tuple-element.9.refs_1_, f32[384,4096]{1,0:T(8,128)S(1)} %get-tuple-element.10.refs_2_, ...), custom_call_target="tpu_custom_call" | custom-call | tf_op jit(solution)/shard_map/write_out/pallas_call | solution.py:409

commit v9 on v5

--- a/solution.py
+++ b/solution.py
@@ -17,6 +17,7 @@
 
 ROWS = 384
 HALF = 192
+GROUPS = ROWS // 8
 COLS = 4096
 DATA = 8
 DEVICES = 16
@@ -47,18 +48,21 @@
     return total
 
 
-def tensor_total(tile):
-    row = [tile[s:s + 1, :] for s in range(8)]
-    first3 = row[0] + row[1] + row[2]
-    first4 = first3 + row[3]
-    mid3 = row[4] + row[5] + row[6]
-    last4 = mid3 + row[7]
+def packed_totals(rows, start, stop):
+    lane = lax.broadcasted_iota(jnp.int32, (8, 128), 1)
     sub = lax.broadcasted_iota(jnp.int32, (8, 128), 0)
-    kind = lax.broadcasted_iota(jnp.int32, (8, 128), 1) % 3
-    full = lambda value: jnp.broadcast_to(value, (8, 128))
-    low = jnp.where(kind == 0, jnp.where(sub == 3, full(row[3]), full(first3)), full(first4))
-    high = jnp.where(kind == 1, jnp.where(sub == 7, full(row[7]), full(mid3)), full(last4))
-    return jnp.where(sub < 4, low, high)
+    value = jnp.where(sub < 4, jnp.broadcast_to(rows[0:1], (8, 128)), jnp.broadcast_to(rows[1:2], (8, 128)))
+    tile = jnp.zeros((8, 128), F32)
+    for group in range(start, stop):
+        low, high = ((3, 4), (4, 7), (4, 8))[group % 3]
+        part = lambda s: (s >= low).astype(jnp.int32) + (s >= high).astype(jnp.int32)
+        same = (lane % 32 == group - start) & (part(sub) == part(sub // 4 * 4 + lane // 32))
+        tile = jnp.where(lane == group, jnp.sum(jnp.where(same, value, 0.0), axis=1, keepdims=True), tile)
+    return tile
+
+
+def packed(tile):
+    return jnp.concatenate([jnp.sum(tile[0:4], axis=0, keepdims=True), jnp.sum(tile[4:8], axis=0, keepdims=True)], axis=0)
 
 
 def first_totals(row):
@@ -141,7 +145,7 @@
             return total + fold_lanes(value * value)
 
         total = lax.fori_loop(0, PIECES, piece, jnp.zeros((8, 128), F32))
-        return jnp.where(lane == group, jnp.sum(total, axis=1, keepdims=True), tile)
+        return jnp.where(lane == 32 * (sub % 4) + group % (GROUPS // 2), jnp.sum(total, axis=1, keepdims=True), tile)
 
 
     def exchange(buf, number):
@@ -200,7 +204,9 @@
             loads[chunk].start()
         if chunk == 1:
             loads[0].wait()
-            weight_buf[linear] = lax.fori_loop(0, ROWS // 8, weight_rows, jnp.zeros((8, 128), F32))
+            for part in range(2):
+                span = (part * (GROUPS // 2), (part + 1) * (GROUPS // 2))
+                weight_buf[linear, 2 * part:2 * part + 2, :] = packed(lax.fori_loop(*span, weight_rows, jnp.zeros((8, 128), F32)))
         if chunk == 2:
             pl.semaphore_wait(plane_sem, 1)
             exchange(weight_buf, EX_WEIGHT)
@@ -232,7 +238,8 @@
         rows = pl.ds(half * HALF, HALF)
         pltpu.make_async_copy(relay.at[rows], relay.at[rows], hop_send.at[half]).wait()
     exchange_wait(weight_buf, ex_recv.at[EX_WEIGHT])
-    weight_norm = jnp.sqrt(tensor_total(gathered(weight_buf)))
+    weights = gathered(weight_buf)
+    weight_norm = jnp.sqrt(packed_totals(weights[0:2], 0, GROUPS // 2) + packed_totals(weights[2:4], GROUPS // 2, GROUPS))
     exchange_wait(norm_buf, ex_recv.at[EX_GRAD])
     grad_norm = jnp.sqrt(jnp.sum(gathered(norm_buf), axis=1, keepdims=True))
     clip = jnp.minimum(1.0, MAX_NORM / grad_norm)
@@ -264,13 +271,15 @@
             tile = jnp.where(lane == place(group), jnp.sum(part_buf[group], axis=1, keepdims=True), tile)
         return tile
 
+    groups = [(start // 8, stop // 8) for start, stop in NORM_CHUNKS]
+
     def step_rates(number):
         if number == 0:
             exchange_wait(first_buf, ex_recv.at[EX_FIRST])
             total = first_totals(gathered(first_buf))
         else:
             exchange_wait(sq_buf.at[number - 1], ex_recv.at[EX_FIRST + number])
-            total = tensor_total(gathered(sq_buf.at[number - 1]))
+            total = packed_totals(gathered(sq_buf.at[number - 1]), *groups[number])
         return weight_norm / jnp.sqrt(total) * LEARN_RATE
 
     def ag_rows(chunk):
@@ -301,18 +310,17 @@
             remote(own, own, ag_send.at[1], ag_y.at[chunk], near_y).start()
             remote(own, own, ag_send.at[2], ag_o, other).start()
 
-    groups = [(start // 8, stop // 8) for start, stop in NORM_CHUNKS]
     adam(*groups[0])
     first_buf[linear] = jnp.sum(row_sums(*groups[0], lambda group: 8 * group + sub), axis=0, keepdims=True)
     adam(groups[1][0], groups[1][0] + 1)
     exchange(first_buf, EX_FIRST)
     adam(groups[1][0] + 1, groups[1][1])
-    sq_buf[0, linear] = row_sums(*groups[1], lambda group: group)
+    sq_buf[0, linear] = packed(row_sums(*groups[1], lambda group: 32 * (sub % 4) + group - groups[1][0]))
     adam(groups[2][0], groups[2][0] + 1)
     exchange(sq_buf.at[0], EX_FIRST + 1)
     update(0, step_rates(0))
     adam(groups[2][0] + 1, groups[2][1])
-    sq_buf[1, linear] = row_sums(*groups[2], lambda group: group)
+    sq_buf[1, linear] = packed(row_sums(*groups[2], lambda group: 32 * (sub % 4) + group - groups[2][0]))
     rates = step_rates(1)
     exchange(sq_buf.at[1], EX_FIRST + 2)
     update(1, rates)
@@ -384,10 +392,10 @@
             scratch_shapes=[
                 pltpu.VMEM((ROWS, COLS), F32),
                 pltpu.VMEM((ROWS, COLS), F32),
-                pltpu.VMEM((DEVICES, 8, 128), F32),
+                pltpu.VMEM((DEVICES, 4, 128), F32),
                 pltpu.VMEM((DEVICES, 1, 128), F32),
                 pltpu.VMEM((DEVICES, 1, 128), F32),
-                pltpu.VMEM((2, DEVICES, 8, 128), F32),
+                pltpu.VMEM((2, DEVICES, 2, 128), F32),
                 pltpu.VMEM((ROWS // 8, 8, 128), F32),
                 dma((3,)),
                 dma((2, RS_CHUNKS)),

time: 337 us -> 336 us (level)
  no operation moved by 1% of the time
where the time goes in v9:
time: 336 us
  Pallas kernels  336 us (100%)
    pallas_call x1, Pallas kernels, device_step(): pl.pallas_call(kernel, name='lamb', out_shape=(pltpu.VMEM((ROWS, DATA * C...  321 us
    pallas_call x1, Pallas kernels, device_step(): pl.pallas_call(write_out, name='write_out', out_shape=[jax.ShapeDtypeStru...  14.2 us

profile of v9, /device:TPU:0, one launch (start us, length us, event | category | flops | bytes accessed | tf_op | source)
XLA Modules:
  0.0 336.3 jit_solution(2628095636509722964)
XLA Ops:
  0.6 321.4 %lamb.1 = (bf16[384,32768]{1,0:T(8,128)(2,1)S(1)}, f32[384,4096]{1,0:T(8,128)S(1)}, f32[384,4096]{1,0:T(8,128)S(1)}, f32[384,4096]{1,0:T(8,128)S(1)}) custom-call(bf16[1,384,32768]{2,1,0:T(8,128)(2,1)} %grad_ref.1, f32[384,4096]{1,0:T(8,128)} %master_ref.1, f32[384,4096]{1,0:T(8,128)} %one_ref.1, f32[384,4096]{1,0:T(8,128)} %two_ref.1), custom_call_target="tpu_custom_call" | custom-call | tf_op jit(solution)/shard_map/lamb/pallas_call | solution.py:386
  322.1 14.2 %write_out.1 = (bf16[384,32768]{1,0:T(8,128)(2,1)}, f32[384,4096]{1,0:T(8,128)}, f32[384,4096]{1,0:T(8,128)}, f32[384,4096]{1,0:T(8,128)}) custom-call(bf16[384,32768]{1,0:T(8,128)(2,1)S(1)} %get-tuple-element.8.refs_0_, f32[384,4096]{1,0:T(8,128)S(1)} %get-tuple-element.9.refs_1_, f32[384,4096]{1,0:T(8,128)S(1)} %get-tuple-element.10.refs_2_, ...), custom_call_target="tpu_custom_call" | custom-call | tf_op jit(solution)/shard_map/write_out/pallas_call | solution.py:417

commit v10 on v9

--- a/solution.py
+++ b/solution.py
@@ -209,7 +209,6 @@
                 weight_buf[linear, 2 * part:2 * part + 2, :] = packed(lax.fori_loop(*span, weight_rows, jnp.zeros((8, 128), F32)))
         if chunk == 2:
             pl.semaphore_wait(plane_sem, 1)
-            exchange(weight_buf, EX_WEIGHT)
             loads[1].wait()
             decay(one, BETA_ONE)
         if chunk == 3:
@@ -234,12 +233,10 @@
 
     norm_buf[linear] = jnp.sum(square, axis=0, keepdims=True)
     exchange(norm_buf, EX_GRAD)
+    exchange(weight_buf, EX_WEIGHT)
     for half in range(2):
         rows = pl.ds(half * HALF, HALF)
         pltpu.make_async_copy(relay.at[rows], relay.at[rows], hop_send.at[half]).wait()
-    exchange_wait(weight_buf, ex_recv.at[EX_WEIGHT])
-    weights = gathered(weight_buf)
-    weight_norm = jnp.sqrt(packed_totals(weights[0:2], 0, GROUPS // 2) + packed_totals(weights[2:4], GROUPS // 2, GROUPS))
     exchange_wait(norm_buf, ex_recv.at[EX_GRAD])
     grad_norm = jnp.sqrt(jnp.sum(gathered(norm_buf), axis=1, keepdims=True))
     clip = jnp.minimum(1.0, MAX_NORM / grad_norm)
@@ -273,7 +270,7 @@
 
     groups = [(start // 8, stop // 8) for start, stop in NORM_CHUNKS]
 
-    def step_rates(number):
+    def step_rates(weight_norm, number):
         if number == 0:
             exchange_wait(first_buf, ex_recv.at[EX_FIRST])
             total = first_totals(gathered(first_buf))
@@ -318,13 +315,16 @@
     sq_buf[0, linear] = packed(row_sums(*groups[1], lambda group: 32 * (sub % 4) + group - groups[1][0]))
     adam(groups[2][0], groups[2][0] + 1)
     exchange(sq_buf.at[0], EX_FIRST + 1)
-    update(0, step_rates(0))
+    exchange_wait(weight_buf, ex_recv.at[EX_WEIGHT])
+    weights = gathered(weight_buf)
+    weight_norm = jnp.sqrt(packed_totals(weights[0:2], 0, GROUPS // 2) + packed_totals(weights[2:4], GROUPS // 2, GROUPS))
+    update(0, step_rates(weight_norm, 0))
     adam(groups[2][0] + 1, groups[2][1])
     sq_buf[1, linear] = packed(row_sums(*groups[2], lambda group: 32 * (sub % 4) + group - groups[2][0]))
-    rates = step_rates(1)
+    rates = step_rates(weight_norm, 1)
     exchange(sq_buf.at[1], EX_FIRST + 2)
     update(1, rates)
-    update(2, step_rates(2))
+    update(2, step_rates(weight_norm, 2))
 
     def arrived(sem, source, rows):
         view = params.at[rows, block(source)]

time: 336 us -> 336 us (level)
  no operation moved by 1% of the time
where the time goes in v10:
time: 336 us
  Pallas kernels  335 us (100%)
    pallas_call x1, Pallas kernels, device_step(): pl.pallas_call(kernel, name='lamb', out_shape=(pltpu.VMEM((ROWS, DATA * C...  321 us
    pallas_call x1, Pallas kernels, device_step(): pl.pallas_call(write_out, name='write_out', out_shape=[jax.ShapeDtypeStru...  14.2 us

profile of v10, /device:TPU:0, one launch (start us, length us, event | category | flops | bytes accessed | tf_op | source)
XLA Modules:
  0.0 336.0 jit_solution(1843484182726211725)
XLA Ops:
  0.6 321.1 %lamb.1 = (bf16[384,32768]{1,0:T(8,128)(2,1)S(1)}, f32[384,4096]{1,0:T(8,128)S(1)}, f32[384,4096]{1,0:T(8,128)S(1)}, f32[384,4096]{1,0:T(8,128)S(1)}) custom-call(bf16[1,384,32768]{2,1,0:T(8,128)(2,1)} %grad_ref.1, f32[384,4096]{1,0:T(8,128)} %master_ref.1, f32[384,4096]{1,0:T(8,128)} %one_ref.1, f32[384,4096]{1,0:T(8,128)} %two_ref.1), custom_call_target="tpu_custom_call" | custom-call | tf_op jit(solution)/shard_map/lamb/pallas_call | solution.py:386
  321.7 14.2 %write_out.1 = (bf16[384,32768]{1,0:T(8,128)(2,1)}, f32[384,4096]{1,0:T(8,128)}, f32[384,4096]{1,0:T(8,128)}, f32[384,4096]{1,0:T(8,128)}) custom-call(bf16[384,32768]{1,0:T(8,128)(2,1)S(1)} %get-tuple-element.8.refs_0_, f32[384,4096]{1,0:T(8,128)S(1)} %get-tuple-element.9.refs_1_, f32[384,4096]{1,0:T(8,128)S(1)} %get-tuple-element.10.refs_2_, ...), custom_call_target="tpu_custom_call" | custom-call | tf_op jit(solution)/shard_map/write_out/pallas_call | solution.py:417

commit v11 on v10

--- a/solution.py
+++ b/solution.py
@@ -24,6 +24,7 @@
 PIECE = 1024
 PIECES = COLS // PIECE
 ADAM_PIECE = 1024
+TAIL = 1024
 OUT_PARTS = 6
 VMEM_LIMIT = 16 << 20
 
@@ -79,7 +80,7 @@
 
 
 def kernel(grad_ref, master_ref, one_ref, two_ref, params, master, one, two, relay, grad, weight_buf, norm_buf, first_buf, sq_buf, part_buf,
-           load_sem, rs_recv, rs_send, hop_recv, hop_send, ex_recv, ex_send, ag_x, ag_y, ag_d, ag_o, ag_send, plane_sem):
+           load_sem, rs_recv, rs_send, hop_recv, hop_send, ex_recv, ex_send, ag_x, ag_y, ag_d, ag_o, ag_send, plane_sem, tail_recv, tail_send, last_recv, last_send):
     model = lax.axis_index("model")
     me = lax.axis_index("data")
     linear = model * DATA + me
@@ -331,22 +332,50 @@
         pltpu.make_async_copy(view, view, sem).wait()
         return view
 
+    def body_of(chunk, source):
+        return params.at[ag_rows(chunk), pl.ds(pl.multiple_of(source * COLS, COLS), COLS - TAIL)]
+
+    def pass_far(chunk, source, direction, target):
+        last = chunk - (AG_CHUNKS - 2)
+        if last < 0:
+            whole = params.at[ag_rows(chunk), block(source)]
+            remote(whole, whole, ag_send.at[direction], ag_d.at[chunk], target).start()
+            return
+        body = body_of(chunk, source)
+        remote(body, body, ag_send.at[direction], ag_d.at[chunk], target).start()
+        tail = params.at[ag_rows(chunk), pl.ds(pl.multiple_of(source * COLS + COLS - TAIL, TAIL), TAIL)]
+        remote(tail, tail, ag_send.at[direction], tail_recv.at[0, last], target).start()
+        remote(tail, tail, tail_send.at[last], tail_recv.at[1, last], target + to_core).start()
+
     for chunk in range(AG_CHUNKS):
         rows = ag_rows(chunk)
         view = arrived(ag_x.at[chunk], near_x, rows)
         if AG_FAR_BY_Y[chunk]:
-            remote(view, view, ag_send.at[1], ag_d.at[chunk], near_y).start()
+            pass_far(chunk, near_x, 1, near_y)
         remote(view, view, ag_send.at[2], ag_o, other).start()
         view = arrived(ag_y.at[chunk], near_y, rows)
         if not AG_FAR_BY_Y[chunk]:
-            remote(view, view, ag_send.at[0], ag_d.at[chunk], near_x).start()
+            pass_far(chunk, near_y, 0, near_x)
         remote(view, view, ag_send.at[2], ag_o, other).start()
 
     for chunk in range(AG_CHUNKS):
-        view = arrived(ag_d.at[chunk], diag, ag_rows(chunk))
-        remote(view, view, ag_send.at[2], ag_o, other).start()
-
-    half_cols = params.at[:, pl.ds(0, DATA // 2 * COLS)]
+        last = chunk - (AG_CHUNKS - 2)
+        if last < 0:
+            view = arrived(ag_d.at[chunk], diag, ag_rows(chunk))
+            remote(view, view, ag_send.at[2], ag_o, other).start()
+        else:
+            view = body_of(chunk, diag)
+            pltpu.make_async_copy(view, view, ag_d.at[chunk]).wait()
+            remote(view, view, last_send.at[last], last_recv.at[last], other).start()
+
+    half_cols = params.at[pl.ds(0, ROWS - 8), pl.ds(0, DATA // 2 * COLS)]
+    for last in range(2):
+        tail = params.at[pl.ds(0, 16), pl.ds(0, TAIL)]
+        for sem in (tail_recv.at[0, last], tail_recv.at[1, last], tail_send.at[last]):
+            pltpu.make_async_copy(tail, tail, sem).wait()
+        body = params.at[pl.ds(0, 16), pl.ds(0, COLS - TAIL)]
+        for sem in (last_recv.at[last], last_send.at[last]):
+            pltpu.make_async_copy(body, body, sem).wait()
     pltpu.make_async_copy(half_cols, half_cols, ag_o).wait()
     pltpu.make_async_copy(half_cols, half_cols, ag_send.at[2]).wait()
     for direction in range(2):
@@ -410,6 +439,10 @@
                 dma,
                 dma((3,)),
                 pltpu.SemaphoreType.REGULAR,
+                dma((2, 2)),
+                dma((2,)),
+                dma((2,)),
+                dma((2,)),
             ],
             compiler_params=pltpu.CompilerParams(collective_id=0, has_side_effects=True, vmem_limit_bytes=VMEM_LIMIT),
         )(local_grads, master, moment_one, moment_two)

time: 336 us -> 336 us (level)
  no operation moved by 1% of the time
where the time goes in v11:
time: 336 us
  Pallas kernels  335 us (100%)
    pallas_call x1, Pallas kernels, device_step(): pl.pallas_call(kernel, name='lamb', out_shape=(pltpu.VMEM((ROWS, DATA * C...  321 us
    pallas_call x1, Pallas kernels, device_step(): pl.pallas_call(write_out, name='write_out', out_shape=[jax.ShapeDtypeStru...  14.2 us

profile of v11, /device:TPU:0, one launch (start us, length us, event | category | flops | bytes accessed | tf_op | source)
XLA Modules:
  0.0 336.0 jit_solution(8668332932911318179)
XLA Ops:
  0.6 321.1 %lamb.1 = (bf16[384,32768]{1,0:T(8,128)(2,1)S(1)}, f32[384,4096]{1,0:T(8,128)S(1)}, f32[384,4096]{1,0:T(8,128)S(1)}, f32[384,4096]{1,0:T(8,128)S(1)}) custom-call(bf16[1,384,32768]{2,1,0:T(8,128)(2,1)} %grad_ref.1, f32[384,4096]{1,0:T(8,128)} %master_ref.1, f32[384,4096]{1,0:T(8,128)} %one_ref.1, f32[384,4096]{1,0:T(8,128)} %two_ref.1), custom_call_target="tpu_custom_call" | custom-call | tf_op jit(solution)/shard_map/lamb/pallas_call | solution.py:415
  321.8 14.2 %write_out.1 = (bf16[384,32768]{1,0:T(8,128)(2,1)}, f32[384,4096]{1,0:T(8,128)}, f32[384,4096]{1,0:T(8,128)}, f32[384,4096]{1,0:T(8,128)}) custom-call(bf16[384,32768]{1,0:T(8,128)(2,1)S(1)} %get-tuple-element.8.refs_0_, f32[384,4096]{1,0:T(8,128)S(1)} %get-tuple-element.9.refs_1_, f32[384,4096]{1,0:T(8,128)S(1)} %get-tuple-element.10.refs_2_, ...), custom_call_target="tpu_custom_call" | custom-call | tf_op jit(solution)/shard_map/write_out/pallas_call | solution.py:450

commit v12 on v10

--- a/solution.py
+++ b/solution.py
@@ -24,7 +24,7 @@
 PIECE = 1024
 PIECES = COLS // PIECE
 ADAM_PIECE = 1024
-OUT_PARTS = 6
+OUT_PARTS = 12
 VMEM_LIMIT = 16 << 20
 
 RS_SIZES = (48, 48, 48, 32, 16)

time: 336 us -> 336 us (level)
  no operation moved by 1% of the time
where the time goes in v12:
time: 336 us
  Pallas kernels  336 us (100%)
    pallas_call x1, Pallas kernels, device_step(): pl.pallas_call(kernel, name='lamb', out_shape=(pltpu.VMEM((ROWS, DATA * C...  321 us
    pallas_call x1, Pallas kernels, device_step(): pl.pallas_call(write_out, name='write_out', out_shape=[jax.ShapeDtypeStru...  14.5 us

profile of v12, /device:TPU:0, one launch (start us, length us, event | category | flops | bytes accessed | tf_op | source)
XLA Modules:
  0.0 336.2 jit_solution(16357283242046610628)
XLA Ops:
  0.6 321.1 %lamb.1 = (bf16[384,32768]{1,0:T(8,128)(2,1)S(1)}, f32[384,4096]{1,0:T(8,128)S(1)}, f32[384,4096]{1,0:T(8,128)S(1)}, f32[384,4096]{1,0:T(8,128)S(1)}) custom-call(bf16[1,384,32768]{2,1,0:T(8,128)(2,1)} %grad_ref.1, f32[384,4096]{1,0:T(8,128)} %master_ref.1, f32[384,4096]{1,0:T(8,128)} %one_ref.1, f32[384,4096]{1,0:T(8,128)} %two_ref.1), custom_call_target="tpu_custom_call" | custom-call | tf_op jit(solution)/shard_map/lamb/pallas_call | solution.py:386
  321.7 14.5 %write_out.1 = (bf16[384,32768]{1,0:T(8,128)(2,1)}, f32[384,4096]{1,0:T(8,128)}, f32[384,4096]{1,0:T(8,128)}, f32[384,4096]{1,0:T(8,128)}) custom-call(bf16[384,32768]{1,0:T(8,128)(2,1)S(1)} %get-tuple-element.8.refs_0_, f32[384,4096]{1,0:T(8,128)S(1)} %get-tuple-element.9.refs_1_, f32[384,4096]{1,0:T(8,128)S(1)} %get-tuple-element.10.refs_2_, ...), custom_call_target="tpu_custom_call" | custom-call | tf_op jit(solution)/shard_map/write_out/pallas_call | solution.py:417
